TPU v7x, 512 devices: a whole 4x8x8 slice. The times are simulated.
512 devices in a mesh: gx: 16 (over y, x_hi), gy: 32 (over z, x_lo, core).
Axes of the slice: x: 4 (x_hi: 2, x_lo: 2; x = x_hi * 2 + x_lo), y: 8, z: 8, core: 2. Of those that a mesh axis runs over, the one named last changes fastest.
Arguments:
- right_side: float32 [262144, 64], P(('gx', 'gy')), may hold values from -6 to 6
- leaf_inverse: float32 [262144, 512], P(('gx', 'gy')), as said below
- basis_one: float32 [262144, 128], P(('gx', 'gy')), may hold values from -0.015625 to 0.015625
- basis_two: float32 [262144, 128], P(('gx', 'gy')), may hold values from -0.0234375 to 0.0234375
- factor_one: bfloat16 [1, 256, 256], replicated, may hold values from -0.5 to 0.5
- factor_two: bfloat16 [2, 256, 256], replicated, may hold values from -0.5 to 0.5
Outputs:
- solution: float32 [262144, 64], P(('gx', 'gy'))
Inputs may be any that keep to these rules, and one draw needn't show every extreme that they name: `leaf_inverse`: each block of 512 consecutive rows is a symmetric positive definite 512 x 512 matrix.
All inputs are finite; a program needn't handle non-finite values.
Results may differ from a plain program's by a relative error of at most 0.0003.
Values sent between devices are 32-bit elements; how exact they have to be, the bound alone decides.
A program may use at most 64 MiB of HBM per device.

v0:
```python
import functools

import jax
import jax.numpy as jnp
from jax import lax
from jax.experimental import pallas as pl
from jax.experimental.pallas import tpu as pltpu
from jax.sharding import PartitionSpec as P

MESH = pl.DeviceIdType.MESH
F32 = jnp.float32
BF16 = jnp.bfloat16
RANK = 128
NZ, NX, NY = 8, 4, 8


def split2(value):
    high = value.astype(BF16)
    return high, (value - high.astype(F32)).astype(BF16)


def dot(left, right, dims):
    return lax.dot_general(left, right, (dims, ((), ())), preferred_element_type=F32)


NN = ((1,), (0,))
TN = ((0,), (0,))


def mm(left, right, dims=NN):
    left_high, left_low = split2(left)
    right_high, right_low = split2(right)
    return dot(left_high, right_high, dims) + (
        dot(left_high, right_low, dims) + dot(left_low, right_high, dims)
    )


def mm_exact_left(left, right, dims=NN):
    right_high, right_low = split2(right)
    return dot(left, right_high, dims) + dot(left, right_low, dims)


def mm_exact_right(left, right, dims=NN):
    left_high, left_low = split2(left)
    return dot(left_high, right, dims) + dot(left_low, right, dims)


def local_kernel(rhs_ref, inv_ref, one_ref, two_ref, prod_ref, s1_ref, s2_ref, x_ref):
    one, two, rhs = one_ref[...], two_ref[...], rhs_ref[...]
    inv = inv_ref[...]
    s2 = mm(inv, two)
    s1 = mm(inv, one)
    x = mm(inv, rhs)
    s1_ref[...] = s1
    s2_ref[...] = s2
    x_ref[...] = x
    prod_ref[0] = mm(two, s2, TN)
    prod_ref[1] = mm(two, s1, TN)
    prod_ref[2] = mm(one, s1, TN)
    prod_ref[3, :, :64] = mm(two, x, TN)
    prod_ref[3, :, 64:] = mm(one, x, TN)


def comm_kernel(
    prod_ref, buf_ref,
    from_core, chip_sum, from_z, z_sum, from_x, x_sum, by_y,
    core_s, core_r, z_s, z_r, x_s, x_r, y_s, y_r,
    gx_s, gx_r, gz_s, gz_r, gc_s, gc_r,
):
    gx, gy = lax.axis_index("gx"), lax.axis_index("gy")
    y, x_hi = lax.div(gx, 2), lax.rem(gx, 2)
    z, x_lo, core = lax.div(gy, 4), lax.rem(lax.div(gy, 2), 2), lax.rem(gy, 2)
    x = x_hi * 2 + x_lo
    other = 1 - core
    sibling = (gx, gy + 1 - 2 * core)

    def z_peer(step):
        there = lax.rem(z + step, NZ)
        return there, (gx, there * 4 + x_lo * 2 + core)

    def x_peer(step):
        there = lax.rem(x + step, NX)
        return there, (y * 2 + lax.div(there, 2), z * 4 + lax.rem(there, 2) * 2 + core)

    def y_peer(step):
        there = lax.rem(y + step, NY)
        return there, (there * 2 + x_hi, gy)

    barrier = pltpu.get_barrier_semaphore()
    peers = [sibling]
    peers += [z_peer(step)[1] for step in range(1, NZ)]
    peers += [x_peer(step)[1] for step in range(1, NX)]
    peers += [y_peer(step)[1] for step in range(1, NY)]
    for peer in peers:
        pl.semaphore_signal(barrier, inc=1, device_id=peer, device_id_type=MESH)
    pl.semaphore_wait(barrier, len(peers))

    def send(source, target, send_sem, recv_sem, peer):
        copy = pltpu.make_async_remote_copy(
            src_ref=source, dst_ref=target, send_sem=send_sem, recv_sem=recv_sem,
            device_id=peer, device_id_type=MESH,
        )
        copy.start()
        return copy

    first = send(prod_ref.at[other], from_core, core_s, core_r, sibling)
    first.wait()
    chip_sum[...] = prod_ref[core] + from_core[...]

    copies = []
    for step in range(1, NZ):
        there, peer = z_peer(step)
        copies.append(send(chip_sum.at[there], from_z.at[step - 1], z_s.at[step - 1], z_r.at[step - 1], peer))
    total = chip_sum[z]
    for step, copy in enumerate(copies):
        copy.wait()
        total = total + from_z[step]
    z_sum[...] = total

    copies = []
    for step in range(1, NX):
        there, peer = x_peer(step)
        copies.append(send(z_sum.at[there], from_x.at[step - 1], x_s.at[step - 1], x_r.at[step - 1], peer))
    total = z_sum[x]
    for step, copy in enumerate(copies):
        copy.wait()
        total = total + from_x[step]
    x_sum[...] = total

    copies = []
    for step in range(1, NY):
        _, peer = y_peer(step)
        copies.append(send(x_sum, by_y.at[y], y_s.at[step - 1], y_r.at[step - 1], peer))
    by_y[y] = total
    for copy in copies:
        copy.wait()
    for slab in range(NY // 2):
        buf_ref[core, z, x, slab] = by_y[2 * slab] + by_y[2 * slab + 1]

    copies = []
    mine = buf_ref.at[core, z, x]
    for step in range(1, NX):
        _, peer = x_peer(step)
        copies.append(send(mine, mine, gx_s.at[step - 1], gx_r.at[step - 1], peer))
    for copy in copies:
        copy.wait()

    copies = []
    plane = buf_ref.at[core, z]
    for step in range(1, NZ):
        _, peer = z_peer(step)
        copies.append(send(plane, plane, gz_s.at[step - 1], gz_r.at[step - 1], peer))
    relays = [send(plane, plane, gc_s.at[0], gc_r.at[0], sibling)]
    for step, copy in enumerate(copies):
        copy.wait()
        origin = lax.rem(z + NZ - (step + 1), NZ)
        part = buf_ref.at[core, origin]
        relays.append(send(part, part, gc_s.at[step + 1], gc_r.at[step + 1], sibling))
    for relay in relays:
        relay.wait()


def sublane():
    return lax.broadcasted_iota(jnp.int32, (8, RANK), 0)


def lane():
    return lax.broadcasted_iota(jnp.int32, (8, RANK), 1)


def row_of(tile, index):
    return jnp.broadcast_to(tile[index : index + 1, :], tile.shape)


def reciprocal(value):
    guess = pl.reciprocal(value, approx=True)
    guess = guess * (2.0 - value * guess)
    return guess * (2.0 - value * guess)


def invert_in_place(work_ref, count):
    def panel_step(panel, carry):
        rows = lax.broadcasted_iota(jnp.int32, (8, RANK), 0)
        lanes = lax.broadcasted_iota(jnp.int32, (8, RANK), 1)
        base = panel * 8
        in_panel = jnp.logical_and(lanes >= base, lanes < base + 8)
        unit = (lanes - base == rows).astype(F32)
        picks = [jnp.full((8, RANK), base + j, jnp.int32) for j in range(8)]
        at = pl.ds(pl.multiple_of(base, 8), 8)
        for which in range(count):
            tile = work_ref[which, at, :]
            cols = [jnp.take_along_axis(tile, picks[j], axis=1) for j in range(8)]
            tile = jnp.where(in_panel, unit, tile)
            scale = jnp.ones((8, RANK), F32)
            for k in range(8):
                inverse = reciprocal(row_of(cols[k], k))
                scale = jnp.where(rows == k, inverse, scale)
                multiplier = jnp.where(rows == k, 0.0, cols[k]) * inverse
                for j in range(k + 1, 8):
                    cols[j] = cols[j] - multiplier * row_of(cols[j], k)
                tile = tile - multiplier * row_of(tile, k)
            tile = tile * scale
            tile_rows = [row_of(tile, j) for j in range(8)]
            for other in range(RANK // 8):
                here = work_ref[which, other * 8 : other * 8 + 8, :]
                update = jnp.where(in_panel, 0.0, here)
                for j in range(8):
                    update = update - jnp.take_along_axis(here, picks[j], axis=1) * tile_rows[j]
                work_ref[which, other * 8 : other * 8 + 8, :] = update
            work_ref[which, at, :] = tile
        return carry

    lax.fori_loop(0, RANK // 8, panel_step, 0)


def solve_kernel(buf_ref, one_ref, two_ref, s1_ref, s2_ref, x_ref, out_ref, work_ref, coef_ref):
    gx = lax.axis_index("gx")
    my_block = lax.div(gx, 4)
    my_pair, my_half = lax.div(my_block, 2), lax.rem(my_block, 2)

    def part(index, slab):
        whole = buf_ref[index // 2, (index % 2) * 4 : (index % 2) * 4 + 4, :, slab]
        return whole.reshape(RANK, RANK)

    def capacitance(factor, grams):
        top = mm_exact_right(grams[0], factor[:RANK])
        low = mm_exact_right(grams[1], factor[RANK:])
        cap = mm_exact_left(factor, jnp.concatenate((top, low), axis=0), TN)
        return cap

    eye = (
        lax.broadcasted_iota(jnp.int32, (RANK, RANK), 0)
        == lax.broadcasted_iota(jnp.int32, (RANK, RANK), 1)
    ).astype(F32)

    def solve(caps, terms, finish):
        count = len(caps)
        for q in range(count):
            work_ref[q] = caps[q][:RANK, :RANK] + eye
        invert_in_place(work_ref, count)
        firsts, crosses, wides, rests = [], [], [], []
        for q in range(count):
            inverse = work_ref[q]
            cross = caps[q][:RANK, RANK:]
            wide = mm(inverse, cross)
            first = mm(inverse, terms[q][:RANK])
            work_ref[q] = caps[q][RANK:, RANK:] + eye - mm(cross, wide, TN)
            rests.append(terms[q][RANK:] - mm(cross, first, TN))
            firsts.append(first)
            wides.append(wide)
        invert_in_place(work_ref, count)
        result = []
        for q in range(count):
            low = mm(work_ref[q], rests[q])
            top = firsts[q] - mm(wides[q], low)
            result.append((top, low))
        return result

    caps, terms = [], []
    for pair in range(2):
        factor = two_ref[pair]
        caps.append(capacitance(factor, [part(0, 2 * pair), part(0, 2 * pair + 1)]))
        sides = [
            jnp.concatenate((part(1, 2 * pair + half), part(3, 2 * pair + half)), axis=1)
            for half in range(2)
        ]
        terms.append(mm_exact_left(factor, jnp.concatenate(sides, axis=0), TN))
    result = solve(caps, terms, None)
    grams, projs = [], []
    for pair in range(2):
        top, low = result[pair]
        coef_ref[pair, :RANK] = top
        coef_ref[pair, RANK:] = low
        term = terms[pair]
        inner = mm(term[:RANK, :RANK], top, TN) + mm(term[RANK:, :RANK], low, TN)
        grams.append(part(2, 2 * pair) + part(2, 2 * pair + 1) - inner[:, :RANK])
        side = part(3, 2 * pair) + part(3, 2 * pair + 1)
        projs.append(side[:, 64:] - inner[:, RANK : RANK + 64])
    factor = one_ref[0]
    cap = capacitance(factor, grams)
    term = mm_exact_left(factor, jnp.concatenate(projs, axis=0), TN)
    ((top, low),) = solve([cap], [term], None)
    coef = jnp.concatenate((top, low), axis=0)
    half_rows = pl.ds(pl.multiple_of(my_pair * RANK, RANK), RANK)
    m1 = mm_exact_left(one_ref[0, half_rows, :], coef)
    own = coef_ref[my_pair]
    inner = own[:, RANK : RANK + 64] - mm(own[:, :RANK], m1)
    block_rows = pl.ds(pl.multiple_of(my_half * RANK, RANK), RANK)
    m2 = mm_exact_left(two_ref[my_pair, block_rows, :], inner)
    out_ref[...] = x_ref[...] - mm(s1_ref[...], m1) - mm(s2_ref[...], m2)


def vmem():
    return pl.BlockSpec(memory_space=pltpu.VMEM)


def body(right_side, leaf_inverse, basis_one, basis_two, factor_one, factor_two):
    rows = right_side.shape[0]
    shape = jax.ShapeDtypeStruct
    prod, s1, s2, x = pl.pallas_call(
        local_kernel,
        out_shape=(
            shape((4, RANK, RANK), F32), shape((rows, RANK), F32),
            shape((rows, RANK), F32), shape((rows, 64), F32),
        ),
        in_specs=[vmem()] * 4,
        out_specs=(vmem(),) * 4,
        compiler_params=pltpu.CompilerParams(vmem_limit_bytes=24 << 20),
    )(right_side, leaf_inverse, basis_one, basis_two)
    dma = pltpu.SemaphoreType.DMA
    buf = pl.pallas_call(
        comm_kernel,
        out_shape=shape((2, NZ, NX, 4, 8, RANK), F32),
        in_specs=[vmem()],
        out_specs=vmem(),
        scratch_shapes=[
            pltpu.VMEM((NZ, NX, 8, RANK), F32),
            pltpu.VMEM((NZ, NX, 8, RANK), F32),
            pltpu.VMEM((NZ - 1, NX, 8, RANK), F32),
            pltpu.VMEM((NX, 8, RANK), F32),
            pltpu.VMEM((NX - 1, 8, RANK), F32),
            pltpu.VMEM((8, RANK), F32),
            pltpu.VMEM((NY, 8, RANK), F32),
            dma, dma, dma((7,)), dma((7,)), dma((3,)), dma((3,)), dma((7,)), dma((7,)),
            dma((3,)), dma((3,)), dma((7,)), dma((7,)), dma((8,)), dma((8,)),
        ],
        compiler_params=pltpu.CompilerParams(
            collective_id=0, has_side_effects=True, vmem_limit_bytes=16 << 20
        ),
    )(prod.reshape(2, NZ, NX, 8, RANK))
    return pl.pallas_call(
        solve_kernel,
        out_shape=shape((rows, 64), F32),
        in_specs=[vmem()] * 6,
        out_specs=vmem(),
        scratch_shapes=[
            pltpu.VMEM((2, RANK, RANK), F32),
            pltpu.VMEM((2, 2 * RANK, 2 * RANK), F32),
        ],
        compiler_params=pltpu.CompilerParams(vmem_limit_bytes=32 << 20),
    )(buf, factor_one, factor_two, s1, s2, x)


def solution(mesh):
    split = P(("gx", "gy"), None)
    return jax.shard_map(
        body, mesh=mesh, in_specs=(split, split, split, split, P(), P()),
        out_specs=split, check_vma=False,
    )
```

profile of v0, /device:TPU:1, one launch (start us, length us, event | category | flops | bytes accessed | tf_op | source)
XLA Modules:
  0.0 100.8 jit_solution(12540492031175988323)
XLA Ops:
  0.0 0.0 copy-start.1
  0.0 1.1 %copy.7.rhs_ref = f32[512,64]{1,0:T(8,128)S(1)} copy(f32[512,64]{0,1:T(8,128)} %param.6) | data formatting | bytes 262144 | tf_op args[0]
  1.1 0.0 copy-done.1
  1.1 0.0 copy-start
  1.1 1.2 %copy-done = f32[512,512]{1,0:T(8,128)S(1)} copy-done((f32[512,512]{1,0:T(8,128)S(1)}, f32[512,512]{1,0:T(8,128)}, u32[]{:S(2)}) %copy-start) | copy-done | bytes 1048600
  2.3 0.0 copy-start.2
  2.3 0.9 copy-done.2
  3.3 2.3 %shard_map.64 = (f32[4,128,128]{2,1,0:T(8,128)S(1)}, f32[512,128]{1,0:T(8,128)S(1)}, f32[512,128]{1,0:T(8,128)S(1)}, f32[512,64]{1,0:T(8,128)S(1)}) custom-call(f32[512,64]{1,0:T(8,128)S(1)} %copy.7.rhs_ref, f32[512,512]{1,0:T(8,128)S(1)} %copy-done, f32[512,128]{1,0:T(8,128)S(1)} %copy-done.1, f32[512,128]{1,0:T(8,128)S(1)} %copy-done.2), custom_call_target="tpu_custom_call" | custom-call | tf_op jit(solution)/shard_map/pallas_call | solution.py:300
  5.5 0.0 copy-start.3
  5.6 0.0 copy-start.4
  5.6 47.6 %shard_map.65.buf_ref = f32[2,8,4,4,8,128]{5,4,3,2,1,0:T(8,128)S(1)} custom-call(f32[2,8,4,8,128]{4,3,2,1,0:T(8,128)S(1)} %bitcast.1), custom_call_target="tpu_custom_call" | custom-call | tf_op jit(solution)/shard_map/pallas_call | solution.py:311
  53.1 0.0 copy-done.3
  53.1 0.0 copy-done.4
  53.2 46.8 %shard_map.66 = f32[512,64]{1,0:T(8,128)S(1)} custom-call(f32[2,8,4,4,8,128]{5,4,3,2,1,0:T(8,128)S(1)} %shard_map.65.buf_ref, bf16[1,256,256]{2,1,0:T(8,128)(2,1)S(1)} %copy-done.4, bf16[2,256,256]{2,1,0:T(8,128)(2,1)S(1)} %copy-done.3, f32[512,128]{1,0:T(8,128)S(1)} %get-tuple-element.10.s1_ref, f32[512,128]{1,0:T(8,128)S(1)} %get-tuple-element.11.s2_ref, ...), custom_call_target="tpu_custom_call" | custom-call | tf_op jit(solution)/shard_map/pallas_call | solution.py:331
  100.0 0.8 copy.8
Async XLA Ops:
  0.0 1.1 %copy-start.1 = (f32[512,128]{1,0:T(8,128)S(1)}, f32[512,128]{1,0:T(8,128)}, u32[]{:S(2)}) copy-start(f32[512,128]{1,0:T(8,128)} %one_ref.2) | copy-start | bytes 786436
  1.1 1.2 %copy-start = (f32[512,512]{1,0:T(8,128)S(1)}, f32[512,512]{1,0:T(8,128)}, u32[]{:S(2)}) copy-start(f32[512,512]{1,0:T(8,128)} %inv_ref.1) | copy-start | bytes 3145732
  2.3 0.9 copy-start.2
  5.5 47.6 %copy-start.3 = (bf16[2,256,256]{2,1,0:T(8,128)(2,1)S(1)}, bf16[2,256,256]{2,1,0:T(8,128)(2,1)}, u32[]{:S(2)}) copy-start(bf16[2,256,256]{2,1,0:T(8,128)(2,1)} %two_ref.3) | copy-start | bytes 786436
  5.6 47.6 %copy-start.4 = (bf16[1,256,256]{2,1,0:T(8,128)(2,1)S(1)}, bf16[1,256,256]{2,1,0:T(8,128)(2,1)}, u32[]{:S(2)}) copy-start(bf16[1,256,256]{2,1,0:T(8,128)(2,1)} %one_ref.3) | copy-start | bytes 393220
where the time goes:
time: 101 us
  Pallas kernels  96.7 us (96%)
  local copies, waits for them, and re-layouts  4.03 us (4%)
    pallas_call x1, Pallas kernels, body(): pl.pallas_call(comm_kernel, out_shape=shape((2, NZ, NX, 4, 8, RANK), F32)...  47.6 us
    pallas_call x1, Pallas kernels, body(): pl.pallas_call(solve_kernel, out_shape=shape((rows, 64), F32), in_specs=[...  46.8 us
    unnamed x11, local copies, waits for them, and re-layouts  3.25 us
    pallas_call x1, Pallas kernels, body(): pl.pallas_call(local_kernel, out_shape=(shape((4, RANK, RANK), F32), shap...  2.27 us

commit v1 on v0

--- a/solution.py
+++ b/solution.py
@@ -178,42 +178,91 @@
     return guess * (2.0 - value * guess)
 
 
-def invert_in_place(work_ref, count):
-    def panel_step(panel, carry):
-        rows = lax.broadcasted_iota(jnp.int32, (8, RANK), 0)
-        lanes = lax.broadcasted_iota(jnp.int32, (8, RANK), 1)
-        base = panel * 8
-        in_panel = jnp.logical_and(lanes >= base, lanes < base + 8)
-        unit = (lanes - base == rows).astype(F32)
-        picks = [jnp.full((8, RANK), base + j, jnp.int32) for j in range(8)]
-        at = pl.ds(pl.multiple_of(base, 8), 8)
+def panel_solve(tiles, cols, unit_rows):
+    scale = [jnp.ones((8, RANK), F32)] * 2
+    cols = [list(pair) for pair in cols]
+    for k in range(16):
+        at, sub = k // 8, k % 8
+        inverse = reciprocal(row_of(cols[k][at], sub))
+        here = unit_rows == sub
+        scale[at] = jnp.where(here, inverse, scale[at])
+        factors = list(cols[k])
+        factors[at] = jnp.where(here, 0.0, factors[at])
+        factors = [factor * inverse for factor in factors]
+        for j in range(k + 1, 16):
+            across = row_of(cols[j][at], sub)
+            cols[j] = [cols[j][t] - factors[t] * across for t in range(2)]
+        across = row_of(tiles[at], sub)
+        tiles = [tiles[t] - factors[t] * across for t in range(2)]
+    return [tiles[t] * scale[t] for t in range(2)]
+
+
+def invert_in_place(work_ref, high_ref, low_ref, count):
+    rows = lax.broadcasted_iota(jnp.int32, (8, RANK), 0)
+    lanes = lax.broadcasted_iota(jnp.int32, (8, RANK), 1)
+    tile_count = RANK // 8
+
+    def apply_last(which, base_before, before):
+        last = jnp.logical_and(lanes >= base_before, lanes < base_before + 16)
+        whole = work_ref[which]
+        left_high, left_low = split2(whole)
+        high, low = high_ref[which], low_ref[which]
+        update = dot(left_high, high, NN) + (dot(left_high, low, NN) + dot(left_low, high, NN))
+        for tile in range(tile_count):
+            at = slice(tile * 8, tile * 8 + 8)
+            work_ref[which, at, :] = jnp.where(last, 0.0, whole[at]) - update[at]
+        at = pl.ds(pl.multiple_of(jnp.maximum(base_before, 0), 16), 16)
+        work_ref[which, at, :] = jnp.concatenate(before, axis=0)
+
+    def step(panel, carry):
+        base = panel * 16
+        inside = jnp.logical_and(lanes >= base, lanes < base + 16)
+        picks = [jnp.full((8, RANK), base + j, jnp.int32) for j in range(16)]
+        following = jnp.minimum(base + 16, RANK - 16)
+        after = []
         for which in range(count):
-            tile = work_ref[which, at, :]
-            cols = [jnp.take_along_axis(tile, picks[j], axis=1) for j in range(8)]
-            tile = jnp.where(in_panel, unit, tile)
-            scale = jnp.ones((8, RANK), F32)
-            for k in range(8):
-                inverse = reciprocal(row_of(cols[k], k))
-                scale = jnp.where(rows == k, inverse, scale)
-                multiplier = jnp.where(rows == k, 0.0, cols[k]) * inverse
-                for j in range(k + 1, 8):
-                    cols[j] = cols[j] - multiplier * row_of(cols[j], k)
-                tile = tile - multiplier * row_of(tile, k)
-            tile = tile * scale
-            tile_rows = [row_of(tile, j) for j in range(8)]
-            for other in range(RANK // 8):
-                here = work_ref[which, other * 8 : other * 8 + 8, :]
-                update = jnp.where(in_panel, 0.0, here)
-                for j in range(8):
-                    update = update - jnp.take_along_axis(here, picks[j], axis=1) * tile_rows[j]
-                work_ref[which, other * 8 : other * 8 + 8, :] = update
-            work_ref[which, at, :] = tile
-        return carry
-
-    lax.fori_loop(0, RANK // 8, panel_step, 0)
-
-
-def solve_kernel(buf_ref, one_ref, two_ref, s1_ref, s2_ref, x_ref, out_ref, work_ref, coef_ref):
+            current, before = carry[which]
+            cols = [
+                [jnp.take_along_axis(current[t], picks[j], axis=1) for t in range(2)]
+                for j in range(16)
+            ]
+            tiles = [
+                jnp.where(inside, (lanes - base == rows + 8 * t).astype(F32), current[t])
+                for t in range(2)
+            ]
+            apply_last(which, base - 16, before)
+            solved = panel_solve(tiles, cols, rows)
+            joined = jnp.concatenate(solved, axis=0)
+            high, low = split2(joined)
+            gone = pl.ds(pl.multiple_of(jnp.maximum(base - 16, 0), 16), 16)
+            high_ref[which, gone, :] = jnp.zeros((16, RANK), BF16)
+            low_ref[which, gone, :] = jnp.zeros((16, RANK), BF16)
+            at = pl.ds(pl.multiple_of(base, 16), 16)
+            high_ref[which, at, :] = high
+            low_ref[which, at, :] = low
+            upcoming = []
+            for t in range(2):
+                tile = work_ref[which, pl.ds(pl.multiple_of(following + 8 * t, 8), 8), :]
+                fresh = jnp.where(inside, 0.0, tile)
+                for j in range(16):
+                    weight = jnp.take_along_axis(tile, picks[j], axis=1)
+                    fresh = fresh - weight * row_of(solved[j // 8], j % 8)
+                upcoming.append(fresh)
+            after.append((tuple(upcoming), tuple(solved)))
+        return tuple(after)
+
+    start = []
+    for which in range(count):
+        high_ref[which] = jnp.zeros((RANK, RANK), BF16)
+        low_ref[which] = jnp.zeros((RANK, RANK), BF16)
+        first = (work_ref[which, :8, :], work_ref[which, 8:16, :])
+        start.append((first, first))
+    done = lax.fori_loop(0, RANK // 16, step, tuple(start))
+    for which in range(count):
+        apply_last(which, RANK - 16, done[which][1])
+
+
+def solve_kernel(buf_ref, one_ref, two_ref, s1_ref, s2_ref, x_ref, out_ref, work_ref, coef_ref, high_ref, low_ref):
     gx = lax.axis_index("gx")
     my_block = lax.div(gx, 4)
     my_pair, my_half = lax.div(my_block, 2), lax.rem(my_block, 2)
@@ -237,7 +286,7 @@
         count = len(caps)
         for q in range(count):
             work_ref[q] = caps[q][:RANK, :RANK] + eye
-        invert_in_place(work_ref, count)
+        invert_in_place(work_ref, high_ref, low_ref, count)
         firsts, crosses, wides, rests = [], [], [], []
         for q in range(count):
             inverse = work_ref[q]
@@ -248,7 +297,7 @@
             rests.append(terms[q][RANK:] - mm(cross, first, TN))
             firsts.append(first)
             wides.append(wide)
-        invert_in_place(work_ref, count)
+        invert_in_place(work_ref, high_ref, low_ref, count)
         result = []
         for q in range(count):
             low = mm(work_ref[q], rests[q])
@@ -328,14 +377,20 @@
             collective_id=0, has_side_effects=True, vmem_limit_bytes=16 << 20
         ),
     )(prod.reshape(2, NZ, NX, 8, RANK))
+    return run_solve(buf, factor_one, factor_two, s1, s2, x)
+
+
+def run_solve(buf, factor_one, factor_two, s1, s2, x):
     return pl.pallas_call(
         solve_kernel,
-        out_shape=shape((rows, 64), F32),
+        out_shape=jax.ShapeDtypeStruct(x.shape, F32),
         in_specs=[vmem()] * 6,
         out_specs=vmem(),
         scratch_shapes=[
             pltpu.VMEM((2, RANK, RANK), F32),
             pltpu.VMEM((2, 2 * RANK, 2 * RANK), F32),
+            pltpu.VMEM((2, RANK, RANK), BF16),
+            pltpu.VMEM((2, RANK, RANK), BF16),
         ],
         compiler_params=pltpu.CompilerParams(vmem_limit_bytes=32 << 20),
     )(buf, factor_one, factor_two, s1, s2, x)

time: 101 us -> 76.3 us (0.76)
  Pallas kernels: 96.7 us -> 72 us
    pallas_call x1, Pallas kernels: 46.8 us -> 22.1 us  [run_solve(): pl.pallas_call(solve_kernel, out_shape=jax.ShapeDtypeStruct(x.shape, F32)...]
where the time goes in v1:
time: 76.3 us; the launch traced here: 76.1 us
  Pallas kernels  72 us (94%)
  local copies, waits for them, and re-layouts  4.03 us (5%)
    pallas_call x1, Pallas kernels, body(): pl.pallas_call(comm_kernel, out_shape=shape((2, NZ, NX, 4, 8, RANK), F32)...  47.6 us
    pallas_call x1, Pallas kernels, run_solve(): pl.pallas_call(solve_kernel, out_shape=jax.ShapeDtypeStruct(x.shape, F32)...  22.1 us
    unnamed x11, local copies, waits for them, and re-layouts  3.25 us
    pallas_call x1, Pallas kernels, body(): pl.pallas_call(local_kernel, out_shape=(shape((4, RANK, RANK), F32), shap...  2.27 us

profile of v1, /device:TPU:1, one launch (start us, length us, event | category | flops | bytes accessed | tf_op | source)
XLA Modules:
  0.0 76.1 jit_solution(4725254616041675823)
XLA Ops:
  0.0 0.0 copy-start.1
  0.0 1.1 %copy.7.rhs_ref = f32[512,64]{1,0:T(8,128)S(1)} copy(f32[512,64]{0,1:T(8,128)} %param.6) | data formatting | bytes 262144 | tf_op args[0]
  1.1 0.0 copy-done.1
  1.1 0.0 copy-start
  1.1 1.2 %copy-done = f32[512,512]{1,0:T(8,128)S(1)} copy-done((f32[512,512]{1,0:T(8,128)S(1)}, f32[512,512]{1,0:T(8,128)}, u32[]{:S(2)}) %copy-start) | copy-done | bytes 1048600
  2.3 0.0 copy-start.2
  2.3 0.9 %copy-done.2 = f32[512,128]{1,0:T(8,128)S(1)} copy-done((f32[512,128]{1,0:T(8,128)S(1)}, f32[512,128]{1,0:T(8,128)}, u32[]{:S(2)}) %copy-start.2) | copy-done | bytes 262168
  3.3 2.3 %shard_map.64 = (f32[4,128,128]{2,1,0:T(8,128)S(1)}, f32[512,128]{1,0:T(8,128)S(1)}, f32[512,128]{1,0:T(8,128)S(1)}, f32[512,64]{1,0:T(8,128)S(1)}) custom-call(f32[512,64]{1,0:T(8,128)S(1)} %copy.7.rhs_ref, f32[512,512]{1,0:T(8,128)S(1)} %copy-done, f32[512,128]{1,0:T(8,128)S(1)} %copy-done.1, f32[512,128]{1,0:T(8,128)S(1)} %copy-done.2), custom_call_target="tpu_custom_call" | custom-call | tf_op jit(solution)/shard_map/pallas_call | solution.py:349
  5.5 0.0 copy-start.3
  5.6 0.0 copy-start.4
  5.6 47.6 %shard_map.65.buf_ref = f32[2,8,4,4,8,128]{5,4,3,2,1,0:T(8,128)S(1)} custom-call(f32[2,8,4,8,128]{4,3,2,1,0:T(8,128)S(1)} %bitcast.1), custom_call_target="tpu_custom_call" | custom-call | tf_op jit(solution)/shard_map/pallas_call | solution.py:360
  53.1 0.0 copy-done.3
  53.1 0.0 copy-done.4
  53.2 22.1 %shard_map.66 = f32[512,64]{1,0:T(8,128)S(1)} custom-call(f32[2,8,4,4,8,128]{5,4,3,2,1,0:T(8,128)S(1)} %shard_map.65.buf_ref, bf16[1,256,256]{2,1,0:T(8,128)(2,1)S(1)} %copy-done.4, bf16[2,256,256]{2,1,0:T(8,128)(2,1)S(1)} %copy-done.3, f32[512,128]{1,0:T(8,128)S(1)} %get-tuple-element.10.s1_ref, f32[512,128]{1,0:T(8,128)S(1)} %get-tuple-element.11.s2_ref, ...), custom_call_target="tpu_custom_call" | custom-call | tf_op jit(solution)/shard_map/pallas_call | solution.py:384
  75.3 0.8 %copy.8 = f32[512,64]{0,1:T(8,128)} copy(f32[512,64]{1,0:T(8,128)S(1)} %shard_map.66) | data formatting | bytes 262144 | tf_op jit(solution)/shard_map/pallas_call | solution.py:384
Async XLA Ops:
  0.0 1.1 %copy-start.1 = (f32[512,128]{1,0:T(8,128)S(1)}, f32[512,128]{1,0:T(8,128)}, u32[]{:S(2)}) copy-start(f32[512,128]{1,0:T(8,128)} %one_ref.2) | copy-start | bytes 786436
  1.1 1.2 %copy-start = (f32[512,512]{1,0:T(8,128)S(1)}, f32[512,512]{1,0:T(8,128)}, u32[]{:S(2)}) copy-start(f32[512,512]{1,0:T(8,128)} %inv_ref.1) | copy-start | bytes 3145732
  2.3 0.9 %copy-start.2 = (f32[512,128]{1,0:T(8,128)S(1)}, f32[512,128]{1,0:T(8,128)}, u32[]{:S(2)}) copy-start(f32[512,128]{1,0:T(8,128)} %two_ref.2) | copy-start | bytes 786436
  5.5 47.6 %copy-start.3 = (bf16[2,256,256]{2,1,0:T(8,128)(2,1)S(1)}, bf16[2,256,256]{2,1,0:T(8,128)(2,1)}, u32[]{:S(2)}) copy-start(bf16[2,256,256]{2,1,0:T(8,128)(2,1)} %two_ref.3) | copy-start | bytes 786436
  5.6 47.6 %copy-start.4 = (bf16[1,256,256]{2,1,0:T(8,128)(2,1)S(1)}, bf16[1,256,256]{2,1,0:T(8,128)(2,1)}, u32[]{:S(2)}) copy-start(bf16[1,256,256]{2,1,0:T(8,128)(2,1)} %one_ref.3) | copy-start | bytes 393220

commit v2 on v1

v2 whole, which is shorter than its diff:
```python
import functools

import jax
import jax.numpy as jnp
from jax import lax
from jax.experimental import pallas as pl
from jax.experimental.pallas import tpu as pltpu
from jax.sharding import PartitionSpec as P

MESH = pl.DeviceIdType.MESH
F32 = jnp.float32
BF16 = jnp.bfloat16
RANK = 128
NZ, NX, NY = 8, 4, 8


def split2(value):
    high = value.astype(BF16)
    return high, (value - high.astype(F32)).astype(BF16)


def dot(left, right, dims):
    return lax.dot_general(left, right, (dims, ((), ())), preferred_element_type=F32)


NN = ((1,), (0,))
TN = ((0,), (0,))
NT = ((1,), (1,))


def mm(left, right, dims=NN):
    left_high, left_low = split2(left)
    right_high, right_low = split2(right)
    return dot(left_high, right_high, dims) + (
        dot(left_high, right_low, dims) + dot(left_low, right_high, dims)
    )


def mm_exact_left(left, right, dims=NN):
    right_high, right_low = split2(right)
    return dot(left, right_high, dims) + dot(left, right_low, dims)


def mm_exact_right(left, right, dims=NN):
    left_high, left_low = split2(left)
    return dot(left_high, right, dims) + dot(left_low, right, dims)


def farthest_first(count):
    return sorted(range(1, count), key=lambda step: -min(step, count - step))


def local_products(inv, two, one, rhs_t, prod_ref, s_high_ref, s_low_ref, x_ref):
    both = jnp.concatenate((two, one), axis=1)
    both_high, both_low = split2(both)
    inv_high, inv_low = split2(inv)
    solved = dot(inv_high, both_high, NN) + (
        dot(inv_high, both_low, NN) + dot(inv_low, both_high, NN)
    )
    rhs_high, rhs_low = split2(rhs_t)
    x_t = dot(rhs_high, inv_high, NN) + (
        dot(rhs_high, inv_low, NN) + dot(rhs_low, inv_high, NN)
    )
    s_high, s_low = split2(solved)
    grams = dot(both_high, s_high, TN) + (dot(both_high, s_low, TN) + dot(both_low, s_high, TN))
    x_high, x_low = split2(x_t)
    projs = dot(x_high, both_high, NN) + (dot(x_high, both_low, NN) + dot(x_low, both_high, NN))
    shape = (2, NZ, 8, RANK)
    prod_ref[0, 0:2] = grams[:RANK, :RANK].reshape(shape)
    prod_ref[0, 2:4] = grams[:RANK, RANK:].reshape(shape)
    prod_ref[1, 0:2] = grams[RANK:, RANK:].reshape(shape)
    prod_ref[1, 2] = projs[:, :RANK].reshape(shape[1:])
    prod_ref[1, 3] = projs[:, RANK:].reshape(shape[1:])
    s_high_ref[...] = s_high
    s_low_ref[...] = s_low
    x_ref[...] = x_t


def gather_kernel(
    rhs_hbm, inv_hbm, one_hbm, two_hbm, buf_ref, s_high_ref, s_low_ref, x_ref,
    rhs_ref, inv_ref, one_ref, two_ref,
    prod_ref, from_core, chip_sum, from_z, z_sum, from_x, x_sum, by_y, away,
    in_s, core_s, core_r, z_s, z_r, x_s, x_r, y_s, y_r, w_s, w_r, gz_s, gz_r, gx_s, gx_r,
):
    gx, gy = lax.axis_index("gx"), lax.axis_index("gy")
    y, x_hi = lax.div(gx, 2), lax.rem(gx, 2)
    z, x_lo, core = lax.div(gy, 4), lax.rem(lax.div(gy, 2), 2), lax.rem(gy, 2)
    x = x_hi * 2 + x_lo
    other = 1 - core
    sibling = (gx, gy + 1 - 2 * core)

    def z_peer(step):
        there = lax.rem(z + step, NZ)
        return there, (gx, there * 4 + x_lo * 2 + core)

    def x_peer(step):
        there = lax.rem(x + step, NX)
        return there, (y * 2 + lax.div(there, 2), z * 4 + lax.rem(there, 2) * 2 + core)

    def y_peer(step):
        there = lax.rem(y + step, NY)
        return there, (there * 2 + x_hi, gy)

    barrier = pltpu.get_barrier_semaphore()
    peers = [z_peer(step)[1] for step in farthest_first(NZ)]
    peers += [y_peer(step)[1] for step in farthest_first(NY)]
    peers += [x_peer(step)[1] for step in farthest_first(NX)]
    peers += [sibling]
    for peer in peers:
        pl.semaphore_signal(barrier, inc=1, device_id=peer, device_id_type=MESH)

    loads = [
        pltpu.make_async_copy(source, target, in_s.at[index])
        for index, (source, target) in enumerate(
            ((inv_hbm, inv_ref), (two_hbm, two_ref), (one_hbm, one_ref), (rhs_hbm, rhs_ref))
        )
    ]
    for load in loads:
        load.start()
    for load in loads:
        load.wait()
    local_products(
        inv_ref[...], two_ref[...], one_ref[...], rhs_ref[...],
        prod_ref, s_high_ref, s_low_ref, x_ref,
    )
    pl.semaphore_wait(barrier, len(peers))

    def send(source, target, send_sem, recv_sem, peer):
        copy = pltpu.make_async_remote_copy(
            src_ref=source, dst_ref=target, send_sem=send_sem, recv_sem=recv_sem,
            device_id=peer, device_id_type=MESH,
        )
        copy.start()
        return copy

    first = send(prod_ref.at[other], from_core, core_s, core_r, sibling)
    first.wait()
    for there in range(NX):
        chip_sum[:, there] = prod_ref[core, there] + from_core[there]

    copies = []
    for step in farthest_first(NZ):
        there, peer = z_peer(step)
        at = step - 1
        copies.append(send(chip_sum.at[there], from_z.at[at], z_s.at[at], z_r.at[at], peer))
    total = chip_sum[z]
    for copy in copies:
        copy.wait()
    for step in range(NZ - 1):
        total = total + from_z[step]
    z_sum[...] = total

    copies = []
    for step in farthest_first(NX):
        there, peer = x_peer(step)
        at = step - 1
        copies.append(send(z_sum.at[there], from_x.at[at], x_s.at[at], x_r.at[at], peer))
    total = z_sum[x]
    for copy in copies:
        copy.wait()
    for step in range(NX - 1):
        total = total + from_x[step]
    x_sum[...] = total

    copies = []
    for step in farthest_first(NY):
        _, peer = y_peer(step)
        copies.append(send(x_sum, by_y.at[y], y_s.at[step - 1], y_r.at[step - 1], peer))
    by_y[y] = total
    for copy in copies:
        copy.wait()
    for slab in range(2):
        here, there = core * 4 + 2 * slab, other * 4 + 2 * slab
        away[slab] = by_y[there] + by_y[there + 1]
        buf_ref[x, z, core, slab] = by_y[here] + by_y[here + 1]
    send(away, buf_ref.at[x, z, core], w_s, w_r, sibling).wait()

    for place, step_peer, count, sends, receives in (
        (buf_ref.at[x, z], z_peer, NZ, gz_s, gz_r),
        (buf_ref.at[x], x_peer, NX, gx_s, gx_r),
    ):
        copies = []
        for step in farthest_first(count):
            _, peer = step_peer(step)
            copies.append(send(place, place, sends.at[step - 1], receives.at[step - 1], peer))
        for copy in copies:
            copy.wait()


def row_of(tile, index):
    return jnp.broadcast_to(tile[index : index + 1, :], tile.shape)


def reciprocal(value):
    guess = pl.reciprocal(value, approx=True)
    guess = guess * (2.0 - value * guess)
    return guess * (2.0 - value * guess)


def panel_solve(tiles, cols, unit_rows):
    scale = [jnp.ones((8, RANK), F32)] * 2
    cols = [list(pair) for pair in cols]
    for k in range(16):
        at, sub = k // 8, k % 8
        inverse = reciprocal(row_of(cols[k][at], sub))
        here = unit_rows == sub
        scale[at] = jnp.where(here, inverse, scale[at])
        factors = list(cols[k])
        factors[at] = jnp.where(here, 0.0, factors[at])
        factors = [factor * inverse for factor in factors]
        for j in range(k + 1, 16):
            across = row_of(cols[j][at], sub)
            cols[j] = [cols[j][t] - factors[t] * across for t in range(2)]
        across = row_of(tiles[at], sub)
        tiles = [tiles[t] - factors[t] * across for t in range(2)]
    return [tiles[t] * scale[t] for t in range(2)]


def invert_in_place(work_ref, high_ref, low_ref, count):
    rows = lax.broadcasted_iota(jnp.int32, (8, RANK), 0)
    lanes = lax.broadcasted_iota(jnp.int32, (8, RANK), 1)
    tile_count = RANK // 8

    def apply_last(which, base_before, before):
        last = jnp.logical_and(lanes >= base_before, lanes < base_before + 16)
        whole = work_ref[which]
        left_high, left_low = split2(whole)
        high, low = high_ref[which], low_ref[which]
        update = dot(left_high, high, NN) + (dot(left_high, low, NN) + dot(left_low, high, NN))
        for tile in range(tile_count):
            at = slice(tile * 8, tile * 8 + 8)
            work_ref[which, at, :] = jnp.where(last, 0.0, whole[at]) - update[at]
        at = pl.ds(pl.multiple_of(jnp.maximum(base_before, 0), 16), 16)
        work_ref[which, at, :] = jnp.concatenate(before, axis=0)

    def step(panel, carry):
        base = panel * 16
        inside = jnp.logical_and(lanes >= base, lanes < base + 16)
        picks = [jnp.full((8, RANK), base + j, jnp.int32) for j in range(16)]
        following = jnp.minimum(base + 16, RANK - 16)
        after = []
        for which in range(count):
            current, before = carry[which]
            cols = [
                [jnp.take_along_axis(current[t], picks[j], axis=1) for t in range(2)]
                for j in range(16)
            ]
            tiles = [
                jnp.where(inside, (lanes - base == rows + 8 * t).astype(F32), current[t])
                for t in range(2)
            ]
            apply_last(which, base - 16, before)
            solved = panel_solve(tiles, cols, rows)
            joined = jnp.concatenate(solved, axis=0)
            high, low = split2(joined)
            gone = pl.ds(pl.multiple_of(jnp.maximum(base - 16, 0), 16), 16)
            high_ref[which, gone, :] = jnp.zeros((16, RANK), BF16)
            low_ref[which, gone, :] = jnp.zeros((16, RANK), BF16)
            at = pl.ds(pl.multiple_of(base, 16), 16)
            high_ref[which, at, :] = high
            low_ref[which, at, :] = low
            upcoming = []
            for t in range(2):
                tile = work_ref[which, pl.ds(pl.multiple_of(following + 8 * t, 8), 8), :]
                fresh = jnp.where(inside, 0.0, tile)
                for j in range(16):
                    weight = jnp.take_along_axis(tile, picks[j], axis=1)
                    fresh = fresh - weight * row_of(solved[j // 8], j % 8)
                upcoming.append(fresh)
            after.append((tuple(upcoming), tuple(solved)))
        return tuple(after)

    start = []
    for which in range(count):
        high_ref[which] = jnp.zeros((RANK, RANK), BF16)
        low_ref[which] = jnp.zeros((RANK, RANK), BF16)
        first = (work_ref[which, :8, :], work_ref[which, 8:16, :])
        start.append((first, first))
    done = lax.fori_loop(0, RANK // 16, step, tuple(start))
    for which in range(count):
        apply_last(which, RANK - 16, done[which][1])


def part(buf_ref, index, slab):
    start = (index % 2) * 2
    return buf_ref[start : start + 2, :, index // 2, slab].reshape(RANK, RANK)


def capacitance(factor, grams):
    top = mm_exact_right(grams[0], factor[:RANK])
    low = mm_exact_right(grams[1], factor[RANK:])
    return mm_exact_left(factor, jnp.concatenate((top, low), axis=0), TN)


def solve(cap, term, work_ref, high_ref, low_ref):
    eye = (
        lax.broadcasted_iota(jnp.int32, (RANK, RANK), 0)
        == lax.broadcasted_iota(jnp.int32, (RANK, RANK), 1)
    ).astype(F32)
    work_ref[0] = cap[:RANK, :RANK] + eye
    invert_in_place(work_ref, high_ref, low_ref, 1)
    inverse = work_ref[0]
    cross = cap[:RANK, RANK:]
    wide = mm(inverse, cross)
    work_ref[0] = cap[RANK:, RANK:] + eye - mm(cross, wide, TN)
    first = mm(inverse, term[:RANK])
    rest = term[RANK:] - mm(cross, first, TN)
    invert_in_place(work_ref, high_ref, low_ref, 1)
    low = mm(work_ref[0], rest)
    top = first - mm(wide, low)
    return top, low


def fine_kernel(buf_ref, two_ref, schur_ref, coef_ref, work_ref, high_ref, low_ref):
    pair = lax.rem(lax.axis_index("gy"), 2)
    factor = two_ref[pair]
    cap = capacitance(factor, [part(buf_ref, 0, 0), part(buf_ref, 0, 1)])
    rights = [part(buf_ref, 3, slab) for slab in range(2)]
    sides = [
        jnp.concatenate((part(buf_ref, 1, slab), rights[slab][:64].T), axis=1)
        for slab in range(2)
    ]
    term = mm_exact_left(factor, jnp.concatenate(sides, axis=0), TN)
    top, low = solve(cap, term, work_ref, high_ref, low_ref)
    coef_ref[:RANK] = top
    coef_ref[RANK:] = low
    inner = mm(term[:RANK, :RANK], top, TN) + mm(term[RANK:, :RANK], low, TN)
    schur_ref[:, :RANK] = part(buf_ref, 2, 0) + part(buf_ref, 2, 1) - inner[:, :RANK]
    schur_ref[:, RANK:] = (rights[0][64:] + rights[1][64:]).T - inner[:, RANK:]


def swap_kernel(schur_ref, coef_ref, schur_out, coef_out, sends, receives):
    gx, gy = lax.axis_index("gx"), lax.axis_index("gy")
    sibling = (gx, gy + 1 - 2 * lax.rem(gy, 2))
    barrier = pltpu.get_barrier_semaphore()
    pl.semaphore_signal(barrier, inc=1, device_id=sibling, device_id_type=MESH)
    pl.semaphore_wait(barrier, 1)
    copies = []
    for index, (source, target) in enumerate(((schur_ref, schur_out), (coef_ref, coef_out))):
        copy = pltpu.make_async_remote_copy(
            src_ref=source, dst_ref=target, send_sem=sends.at[index],
            recv_sem=receives.at[index], device_id=sibling, device_id_type=MESH,
        )
        copy.start()
        copies.append(copy)
    for copy in copies:
        copy.wait()


def coarse_kernel(
    schur_ref, coef_ref, schur_other, coef_other, one_ref, two_ref, s_high_ref, s_low_ref, x_ref,
    out_ref, schurs, coefs, work_ref, high_ref, low_ref,
):
    block = lax.div(lax.axis_index("gx"), 4)
    my_pair, my_half = lax.div(block, 2), lax.rem(block, 2)
    core = lax.rem(lax.axis_index("gy"), 2)
    schurs[core] = schur_ref[...]
    schurs[1 - core] = schur_other[...]
    coefs[core] = coef_ref[...]
    coefs[1 - core] = coef_other[...]
    factor = one_ref[0]
    cap = capacitance(factor, [schurs[0, :, :RANK], schurs[1, :, :RANK]])
    term = mm_exact_left(
        factor, jnp.concatenate((schurs[0, :, RANK:], schurs[1, :, RANK:]), axis=0), TN
    )
    top, low = solve(cap, term, work_ref, high_ref, low_ref)
    half_rows = pl.ds(pl.multiple_of(my_pair * RANK, RANK), RANK)
    m1 = mm_exact_left(one_ref[0, half_rows, :], jnp.concatenate((top, low), axis=0))
    own = coefs[my_pair]
    inner = own[:, RANK:] - mm(own[:, :RANK], m1)
    block_rows = pl.ds(pl.multiple_of(my_half * RANK, RANK), RANK)
    m2 = mm_exact_left(two_ref[my_pair, block_rows, :], inner)
    weights = jnp.concatenate((m2, m1), axis=0).T
    w_high, w_low = split2(weights)
    s_high = s_high_ref[...]
    out_ref[...] = x_ref[...] - (
        dot(w_high, s_high, NT) + (dot(w_high, s_low_ref[...], NT) + dot(w_low, s_high, NT))
    )


def vmem():
    return pl.BlockSpec(memory_space=pltpu.VMEM)


def shape(*dims, kind=F32):
    return jax.ShapeDtypeStruct(dims, kind)


def inverse_scratch():
    return [
        pltpu.VMEM((1, RANK, RANK), F32),
        pltpu.VMEM((1, RANK, RANK), BF16),
        pltpu.VMEM((1, RANK, RANK), BF16),
    ]


def run_gather(rhs_t, leaf_inverse, basis_one, basis_two):
    rows = leaf_inverse.shape[0]
    dma = pltpu.SemaphoreType.DMA
    return pl.pallas_call(
        gather_kernel,
        out_shape=(
            shape(NX, NZ, 2, 2, 8, RANK), shape(rows, 2 * RANK, kind=BF16),
            shape(rows, 2 * RANK, kind=BF16), shape(64, rows),
        ),
        in_specs=[pl.BlockSpec(memory_space=pltpu.HBM)] * 4,
        out_specs=(vmem(),) * 4,
        scratch_shapes=[
            pltpu.VMEM((64, rows), F32),
            pltpu.VMEM((rows, rows), F32),
            pltpu.VMEM((rows, RANK), F32),
            pltpu.VMEM((rows, RANK), F32),
            pltpu.VMEM((2, NX, NZ, 8, RANK), F32),
            pltpu.VMEM((NX, NZ, 8, RANK), F32),
            pltpu.VMEM((NZ, NX, 8, RANK), F32),
            pltpu.VMEM((NZ - 1, NX, 8, RANK), F32),
            pltpu.VMEM((NX, 8, RANK), F32),
            pltpu.VMEM((NX - 1, 8, RANK), F32),
            pltpu.VMEM((8, RANK), F32),
            pltpu.VMEM((NY, 8, RANK), F32),
            pltpu.VMEM((2, 8, RANK), F32),
            dma((4,)), dma, dma, dma((7,)), dma((7,)), dma((3,)), dma((3,)), dma((7,)), dma((7,)),
            dma, dma, dma((7,)), dma((7,)), dma((3,)), dma((3,)),
        ],
        compiler_params=pltpu.CompilerParams(
            collective_id=0, has_side_effects=True, vmem_limit_bytes=62 << 20
        ),
    )(rhs_t, leaf_inverse, basis_one, basis_two)


def run_fine(buf, factor_two):
    return pl.pallas_call(
        fine_kernel,
        out_shape=(shape(RANK, 192), shape(2 * RANK, 192)),
        in_specs=[vmem()] * 2,
        out_specs=(vmem(),) * 2,
        scratch_shapes=inverse_scratch(),
        compiler_params=pltpu.CompilerParams(vmem_limit_bytes=32 << 20),
    )(buf, factor_two)


def run_swap(schur, coef):
    dma = pltpu.SemaphoreType.DMA
    return pl.pallas_call(
        swap_kernel,
        out_shape=(shape(*schur.shape), shape(*coef.shape)),
        in_specs=[vmem()] * 2,
        out_specs=(vmem(),) * 2,
        scratch_shapes=[dma((2,)), dma((2,))],
        compiler_params=pltpu.CompilerParams(
            collective_id=1, has_side_effects=True, vmem_limit_bytes=16 << 20
        ),
    )(schur, coef)


def run_coarse(schur, coef, schur_other, coef_other, factor_one, factor_two, s_high, s_low, x_t):
    return pl.pallas_call(
        coarse_kernel,
        out_shape=shape(*x_t.shape),
        in_specs=[vmem()] * 9,
        out_specs=vmem(),
        scratch_shapes=[
            pltpu.VMEM((2, RANK, 192), F32),
            pltpu.VMEM((2, 2 * RANK, 192), F32),
        ] + inverse_scratch(),
        compiler_params=pltpu.CompilerParams(vmem_limit_bytes=32 << 20),
    )(schur, coef, schur_other, coef_other, factor_one, factor_two, s_high, s_low, x_t)


def body(right_side, leaf_inverse, basis_one, basis_two, factor_one, factor_two):
    buf, s_high, s_low, x_t = run_gather(right_side.T, leaf_inverse, basis_one, basis_two)
    schur, coef = run_fine(buf, factor_two)
    schur_other, coef_other = run_swap(schur, coef)
    out_t = run_coarse(
        schur, coef, schur_other, coef_other, factor_one, factor_two, s_high, s_low, x_t
    )
    return out_t.T


def solution(mesh):
    split = P(("gx", "gy"), None)
    return jax.shard_map(
        body, mesh=mesh, in_specs=(split, split, split, split, P(), P()),
        out_specs=split, check_vma=False,
    )
```

time: 76.3 us -> 67.6 us (0.89)
  Pallas kernels: 72 us -> 66.3 us
  local copies, waits for them, and re-layouts: 4.03 us -> 1.06 us
    pallas_call x3 -> x4, Pallas kernels: 72 us -> 66.3 us  [the longest x1 46.2 us: run_gather(): pl.pallas_call(gather_kernel, out_shape=(shape(NX, NZ, 2, 2, 8, RANK), sh...]
    unnamed x11 -> x12, local copies, waits for them, and re-layouts: 3.25 us -> 1.06 us
    pallas_call x1 -> x0, local copies, waits for them, and re-layouts: 0.77 us -> none  [run_solve(): pl.pallas_call(solve_kernel, out_shape=jax.ShapeDtypeStruct(x.shape, F32)...]
where the time goes in v2:
time: 67.6 us; the launch traced here: 67.4 us
  Pallas kernels  66.3 us (98%)
  local copies, waits for them, and re-layouts  1.06 us (2%)
    pallas_call x1, Pallas kernels, run_gather(): pl.pallas_call(gather_kernel, out_shape=(shape(NX, NZ, 2, 2, 8, RANK), sh...  46.2 us
    pallas_call x1, Pallas kernels, run_coarse(): pl.pallas_call(coarse_kernel, out_shape=shape(*x_t.shape), in_specs=[vmem...  9.1 us
    pallas_call x1, Pallas kernels, run_fine(): pl.pallas_call(fine_kernel, out_shape=(shape(RANK, 192), shape(2 * RANK,...  7.96 us
    pallas_call x1, Pallas kernels, run_swap(): pl.pallas_call(swap_kernel, out_shape=(shape(*schur.shape), shape(*coef.s...  3 us

profile of v2, /device:TPU:1, one launch (start us, length us, event | category | flops | bytes accessed | tf_op | source)
XLA Modules:
  0.0 67.4 jit_solution(10956016108862141063)
XLA Ops:
  0.0 0.0 copy-start
  0.0 46.2 %shard_map.64 = (f32[4,8,2,2,8,128]{5,4,3,2,1,0:T(8,128)}, bf16[512,256]{1,0:T(8,128)(2,1)}, bf16[512,256]{1,0:T(8,128)(2,1)}, f32[64,512]{1,0:T(8,128)}) custom-call(f32[64,512]{1,0:T(8,128)} %bitcast.2, f32[512,512]{1,0:T(8,128)} %inv_hbm.1, f32[512,128]{1,0:T(8,128)} %one_hbm.1, f32[512,128]{1,0:T(8,128)} %two_hbm.1), custom_call_target="tpu_custom_call" | custom-call | tf_op jit(solution)/shard_map/pallas_call | solution.py:400
  46.2 0.0 copy-done
  46.2 0.0 copy-start.1
  46.2 1.0 %copy-done.1 = f32[4,8,2,2,8,128]{5,4,3,2,1,0:T(8,128)S(1)} copy-done((f32[4,8,2,2,8,128]{5,4,3,2,1,0:T(8,128)S(1)}, f32[4,8,2,2,8,128]{5,4,3,2,1,0:T(8,128)}, u32[]{:S(2)}) %copy-start.1) | copy-done | bytes 524312
  47.3 0.0 copy-start.3
  47.3 0.0 copy-start.5
  47.3 8.0 %shard_map.65 = (f32[128,192]{1,0:T(8,128)S(1)}, f32[256,192]{1,0:T(8,128)S(1)}) custom-call(f32[4,8,2,2,8,128]{5,4,3,2,1,0:T(8,128)S(1)} %copy-done.1, bf16[2,256,256]{2,1,0:T(8,128)(2,1)S(1)} %copy-done), custom_call_target="tpu_custom_call" | custom-call | tf_op jit(solution)/shard_map/pallas_call | solution.py:432
  55.3 0.0 copy-start.2
  55.3 0.0 copy-start.4
  55.3 3.0 %shard_map.66 = (f32[128,192]{1,0:T(8,128)S(1)}, f32[256,192]{1,0:T(8,128)S(1)}) custom-call(f32[128,192]{1,0:T(8,128)S(1)} %get-tuple-element.14.schur_ref, f32[256,192]{1,0:T(8,128)S(1)} %get-tuple-element.15.coef_ref), custom_call_target="tpu_custom_call" | custom-call | tf_op jit(solution)/shard_map/pallas_call | solution.py:444
  58.3 0.0 copy-done.3
  58.3 0.0 copy-done.5
  58.3 0.0 copy-done.2
  58.3 0.0 copy-done.4
  58.3 9.1 %shard_map.67 = f32[64,512]{1,0:T(8,128)} custom-call(f32[128,192]{1,0:T(8,128)S(1)} %get-tuple-element.14.schur_ref, f32[256,192]{1,0:T(8,128)S(1)} %get-tuple-element.15.coef_ref, f32[128,192]{1,0:T(8,128)S(1)} %get-tuple-element.16.schur_other, f32[256,192]{1,0:T(8,128)S(1)} %get-tuple-element.17.coef_other, bf16[1,256,256]{2,1,0:T(8,128)(2,1)S(1)} %copy-done.4, ...), custom_call_target="tpu_custom_call" | custom-call | tf_op jit(solution)/shard_map/pallas_call | solution.py:457
Async XLA Ops:
  0.0 46.2 %copy-start = (bf16[2,256,256]{2,1,0:T(8,128)(2,1)S(1)}, bf16[2,256,256]{2,1,0:T(8,128)(2,1)}, u32[]{:S(2)}) copy-start(bf16[2,256,256]{2,1,0:T(8,128)(2,1)} %two_ref.3) | copy-start | bytes 786436
  46.2 1.0 %copy-start.1 = (f32[4,8,2,2,8,128]{5,4,3,2,1,0:T(8,128)S(1)}, f32[4,8,2,2,8,128]{5,4,3,2,1,0:T(8,128)}, u32[]{:S(2)}) copy-start(f32[4,8,2,2,8,128]{5,4,3,2,1,0:T(8,128)} %get-tuple-element.13.buf_ref) | copy-start | bytes 1572868
  47.3 11.0 %copy-start.3 = (bf16[512,256]{1,0:T(8,128)(2,1)S(1)}, bf16[512,256]{1,0:T(8,128)(2,1)}, u32[]{:S(2)}) copy-start(bf16[512,256]{1,0:T(8,128)(2,1)} %get-tuple-element.19.s_low_ref) | copy-start | bytes 786436
  47.3 11.0 %copy-start.5 = (f32[64,512]{1,0:T(8,128)S(1)}, f32[64,512]{1,0:T(8,128)}, u32[]{:S(2)}) copy-start(f32[64,512]{1,0:T(8,128)} %get-tuple-element.20.x_ref) | copy-start | bytes 393220
  55.3 3.1 %copy-start.2 = (bf16[512,256]{1,0:T(8,128)(2,1)S(1)}, bf16[512,256]{1,0:T(8,128)(2,1)}, u32[]{:S(2)}) copy-start(bf16[512,256]{1,0:T(8,128)(2,1)} %get-tuple-element.18.s_high_ref) | copy-start | bytes 786436
  55.3 3.1 %copy-start.4 = (bf16[1,256,256]{2,1,0:T(8,128)(2,1)S(1)}, bf16[1,256,256]{2,1,0:T(8,128)(2,1)}, u32[]{:S(2)}) copy-start(bf16[1,256,256]{2,1,0:T(8,128)(2,1)} %one_ref.1) | copy-start | bytes 393220

commit v3 on v2

v3 whole, which is shorter than its diff:
```python
import functools

import jax
import jax.numpy as jnp
from jax import lax
from jax.experimental import pallas as pl
from jax.experimental.pallas import tpu as pltpu
from jax.sharding import PartitionSpec as P

MESH = pl.DeviceIdType.MESH
F32 = jnp.float32
BF16 = jnp.bfloat16
RANK = 128
NZ, NX, NY = 8, 4, 8


def split2(value):
    high = value.astype(BF16)
    return high, (value - high.astype(F32)).astype(BF16)


def dot(left, right, dims):
    return lax.dot_general(left, right, (dims, ((), ())), preferred_element_type=F32)


NN = ((1,), (0,))
TN = ((0,), (0,))
NT = ((1,), (1,))


def mm(left, right, dims=NN):
    left_high, left_low = split2(left)
    right_high, right_low = split2(right)
    return dot(left_high, right_high, dims) + (
        dot(left_high, right_low, dims) + dot(left_low, right_high, dims)
    )


def mm_exact_left(left, right, dims=NN):
    right_high, right_low = split2(right)
    return dot(left, right_high, dims) + dot(left, right_low, dims)


def mm_exact_right(left, right, dims=NN):
    left_high, left_low = split2(left)
    return dot(left_high, right, dims) + dot(left_low, right, dims)


def away(step, count):
    return min(step, count - step)


def farthest_first(count):
    return sorted(range(1, count), key=lambda step: -away(step, count))


def plane_steps():
    steps = [(up, over) for up in range(NZ) for over in range(NX) if up or over]
    return sorted(steps, key=lambda step: -away(step[0], NZ) - away(step[1], NX))


def local_products(inv, two, one, rhs_t, prod_ref, s_high_ref, s_low_ref, x_ref):
    both = jnp.concatenate((two, one), axis=1)
    both_high, both_low = split2(both)
    inv_high, inv_low = split2(inv)
    solved = dot(inv_high, both_high, NN) + (
        dot(inv_high, both_low, NN) + dot(inv_low, both_high, NN)
    )
    rhs_high, rhs_low = split2(rhs_t)
    x_t = dot(rhs_high, inv_high, NN) + (
        dot(rhs_high, inv_low, NN) + dot(rhs_low, inv_high, NN)
    )
    s_high, s_low = split2(solved)
    grams = dot(both_high, s_high, TN) + (dot(both_high, s_low, TN) + dot(both_low, s_high, TN))
    x_high, x_low = split2(x_t)
    projs = dot(x_high, both_high, NN) + (dot(x_high, both_low, NN) + dot(x_low, both_high, NN))
    shape = (2, NZ, 8, RANK)
    prod_ref[0, 0:2] = grams[:RANK, :RANK].reshape(shape)
    prod_ref[0, 2:4] = grams[:RANK, RANK:].reshape(shape)
    prod_ref[1, 0:2] = grams[RANK:, RANK:].reshape(shape)
    prod_ref[1, 2] = projs[:, :RANK].reshape(shape[1:])
    prod_ref[1, 3] = projs[:, RANK:].reshape(shape[1:])
    s_high_ref[...] = s_high
    s_low_ref[...] = s_low
    x_ref[...] = x_t


def whole_kernel(
    rhs_hbm, inv_hbm, one_hbm, two_hbm, coarse_hbm, fine_hbm, out_ref,
    s_high_ref, s_low_ref, x_ref, schur_ref, coef_ref,
    rhs_ref, inv_ref, one_ref, two_ref, buf_ref,
    prod_ref, from_core, chip_sum, from_plane, x_sum, by_y, leaving,
    work_ref, high_ref, low_ref, coarse_ref, fine_ref,
    in_s, core_s, core_r, p_s, p_r, y_s, y_r, w_s, w_r, gz_s, gz_r, gx_s, gx_r, o_s, o_r,
):
    gx, gy = lax.axis_index("gx"), lax.axis_index("gy")
    y, x_hi = lax.div(gx, 2), lax.rem(gx, 2)
    z, x_lo, core = lax.div(gy, 4), lax.rem(lax.div(gy, 2), 2), lax.rem(gy, 2)
    x = x_hi * 2 + x_lo
    other = 1 - core
    sibling = (gx, gy + 1 - 2 * core)

    def plane_peer(up, over):
        z_there, x_there = lax.rem(z + up, NZ), lax.rem(x + over, NX)
        gx_there = y * 2 + lax.div(x_there, 2)
        return z_there, x_there, (gx_there, z_there * 4 + lax.rem(x_there, 2) * 2 + core)

    def z_peer(step):
        there = lax.rem(z + step, NZ)
        return there, (gx, there * 4 + x_lo * 2 + core)

    def x_peer(step):
        there = lax.rem(x + step, NX)
        return there, (y * 2 + lax.div(there, 2), z * 4 + lax.rem(there, 2) * 2 + core)

    def y_peer(step):
        there = lax.rem(y + step, NY)
        return there, (there * 2 + x_hi, gy)

    barrier = pltpu.get_barrier_semaphore()
    peers = [plane_peer(up, over)[2] for up, over in plane_steps()]
    peers += [y_peer(step)[1] for step in farthest_first(NY)]
    peers += [sibling]
    for peer in peers:
        pl.semaphore_signal(barrier, inc=1, device_id=peer, device_id_type=MESH)

    loads = [
        pltpu.make_async_copy(source, target, in_s.at[index])
        for index, (source, target) in enumerate(
            ((inv_hbm, inv_ref), (two_hbm, two_ref), (one_hbm, one_ref), (rhs_hbm, rhs_ref),
             (fine_hbm, fine_ref), (coarse_hbm, coarse_ref))
        )
    ]
    for load in loads:
        load.start()
    for load in loads[:4]:
        load.wait()
    local_products(
        inv_ref[...], two_ref[...], one_ref[...], rhs_ref[...],
        prod_ref, s_high_ref, s_low_ref, x_ref,
    )
    pl.semaphore_wait(barrier, len(peers))

    def send(source, target, send_sem, recv_sem, peer):
        copy = pltpu.make_async_remote_copy(
            src_ref=source, dst_ref=target, send_sem=send_sem, recv_sem=recv_sem,
            device_id=peer, device_id_type=MESH,
        )
        copy.start()
        return copy

    first = send(prod_ref.at[other], from_core, core_s, core_r, sibling)
    first.wait()
    for there in range(NX):
        chip_sum[:, there] = prod_ref[core, there] + from_core[there]

    copies = []
    for up, over in plane_steps():
        z_there, x_there, peer = plane_peer(up, over)
        at = up * NX + over - 1
        copies.append(
            send(chip_sum.at[z_there, x_there], from_plane.at[at], p_s.at[at], p_r.at[at], peer)
        )
    total = chip_sum[z, x]
    for copy in copies:
        copy.wait()
    for at in range(NZ * NX - 1):
        total = total + from_plane[at]
    x_sum[...] = total

    copies = []
    for step in farthest_first(NY):
        _, peer = y_peer(step)
        copies.append(send(x_sum, by_y.at[y], y_s.at[step - 1], y_r.at[step - 1], peer))
    by_y[y] = total
    for copy in copies:
        copy.wait()
    for slab in range(2):
        here, there = core * 4 + 2 * slab, other * 4 + 2 * slab
        leaving[slab] = by_y[there] + by_y[there + 1]
        buf_ref[x, z, core, slab] = by_y[here] + by_y[here + 1]
    send(leaving, buf_ref.at[x, z, core], w_s, w_r, sibling).wait()

    copies = []
    place = buf_ref.at[x, z]
    for step in farthest_first(NZ):
        _, peer = z_peer(step)
        copies.append(send(place, place, gz_s.at[step - 1], gz_r.at[step - 1], peer))
    for copy in copies:
        copy.wait()

    waves = []
    for wave in range(2):
        place = buf_ref.at[x, :, wave]
        copies = []
        for step in farthest_first(NX):
            _, peer = x_peer(step)
            at = wave * 3 + step - 1
            copies.append(send(place, place, gx_s.at[at], gx_r.at[at], peer))
        waves.append(copies)
    for copy in waves[0]:
        copy.wait()

    for load in loads[4:]:
        load.wait()
    factor = fine_ref[core]
    cap = capacitance(factor, [part(buf_ref, 0, 0), part(buf_ref, 0, 1)])
    mixed = jnp.concatenate((part(buf_ref, 1, 0), part(buf_ref, 1, 1)), axis=0)
    coarse_term = mm_exact_left(factor, mixed, TN)
    eye = identity()
    work_ref[0] = cap[:RANK, :RANK] + eye
    invert_in_place(work_ref, high_ref, low_ref, 1)
    for copy in waves[1]:
        copy.wait()
    rights = [part(buf_ref, 3, slab) for slab in range(2)]
    right = jnp.concatenate([rights[slab][:64].T for slab in range(2)], axis=0)
    term = jnp.concatenate((coarse_term, mm_exact_left(factor, right, TN)), axis=1)
    top, low = finish_solve(cap, term, work_ref, high_ref, low_ref)
    inner = mm(term[:RANK, :RANK], top, TN) + mm(term[RANK:, :RANK], low, TN)
    coef_ref[core, :RANK] = top
    coef_ref[core, RANK:] = low
    schur_ref[core, :, :RANK] = part(buf_ref, 2, 0) + part(buf_ref, 2, 1) - inner[:, :RANK]
    schur_ref[core, :, RANK:] = (rights[0][64:] + rights[1][64:]).T - inner[:, RANK:]
    swaps = [
        send(ref.at[core], ref.at[core], o_s.at[at], o_r.at[at], sibling)
        for at, ref in enumerate((schur_ref, coef_ref))
    ]
    for swap in swaps:
        swap.wait()

    block = lax.div(gx, 4)
    my_pair, my_half = lax.div(block, 2), lax.rem(block, 2)
    factor = coarse_ref[0]
    cap = capacitance(factor, [schur_ref[0, :, :RANK], schur_ref[1, :, :RANK]])
    term = mm_exact_left(
        factor, jnp.concatenate((schur_ref[0, :, RANK:], schur_ref[1, :, RANK:]), axis=0), TN
    )
    work_ref[0] = cap[:RANK, :RANK] + identity()
    invert_in_place(work_ref, high_ref, low_ref, 1)
    top, low = finish_solve(cap, term, work_ref, high_ref, low_ref)
    half_rows = pl.ds(pl.multiple_of(my_pair * RANK, RANK), RANK)
    m1 = mm_exact_left(coarse_ref[0, half_rows, :], jnp.concatenate((top, low), axis=0))
    own = coef_ref[my_pair]
    inner = own[:, RANK:] - mm(own[:, :RANK], m1)
    block_rows = pl.ds(pl.multiple_of(my_half * RANK, RANK), RANK)
    m2 = mm_exact_left(fine_ref[my_pair, block_rows, :], inner)
    weights = jnp.concatenate((m2, m1), axis=0).T
    w_high, w_low = split2(weights)
    s_high = s_high_ref[...]
    out_ref[...] = x_ref[...] - (
        dot(w_high, s_high, NT) + (dot(w_high, s_low_ref[...], NT) + dot(w_low, s_high, NT))
    )


def row_of(tile, index):
    return jnp.broadcast_to(tile[index : index + 1, :], tile.shape)


def reciprocal(value):
    guess = pl.reciprocal(value, approx=True)
    guess = guess * (2.0 - value * guess)
    return guess * (2.0 - value * guess)


def panel_solve(tiles, cols, unit_rows):
    scale = [jnp.ones((8, RANK), F32)] * 2
    cols = [list(pair) for pair in cols]
    for k in range(16):
        at, sub = k // 8, k % 8
        inverse = reciprocal(row_of(cols[k][at], sub))
        here = unit_rows == sub
        scale[at] = jnp.where(here, inverse, scale[at])
        factors = list(cols[k])
        factors[at] = jnp.where(here, 0.0, factors[at])
        factors = [factor * inverse for factor in factors]
        for j in range(k + 1, 16):
            across = row_of(cols[j][at], sub)
            cols[j] = [cols[j][t] - factors[t] * across for t in range(2)]
        across = row_of(tiles[at], sub)
        tiles = [tiles[t] - factors[t] * across for t in range(2)]
    return [tiles[t] * scale[t] for t in range(2)]


def invert_in_place(work_ref, high_ref, low_ref, count):
    rows = lax.broadcasted_iota(jnp.int32, (8, RANK), 0)
    lanes = lax.broadcasted_iota(jnp.int32, (8, RANK), 1)
    tile_count = RANK // 8

    def apply_last(which, base_before, place, before):
        last = jnp.logical_and(lanes >= base_before, lanes < base_before + 16)
        whole = work_ref[which]
        left_high, left_low = split2(whole)
        high, low = high_ref[which], low_ref[which]
        update = dot(left_high, high, NN) + (dot(left_high, low, NN) + dot(left_low, high, NN))
        for tile in range(tile_count):
            at = slice(tile * 8, tile * 8 + 8)
            work_ref[which, at, :] = jnp.where(last, 0.0, whole[at]) - update[at]
        work_ref[which, place, :] = jnp.concatenate(before, axis=0)

    def step(panel, carry):
        base = panel * 16
        inside = jnp.logical_and(lanes >= base, lanes < base + 16)
        picks = [jnp.full((8, RANK), base + j, jnp.int32) for j in range(16)]
        following = lax.rem(base + 16, RANK)
        gone = pl.ds(pl.multiple_of(lax.rem(base + RANK - 16, RANK), 16), 16)
        after = []
        for which in range(count):
            current, before = carry[which]
            cols = [
                [jnp.take_along_axis(current[t], picks[j], axis=1) for t in range(2)]
                for j in range(16)
            ]
            tiles = [
                jnp.where(inside, (lanes - base == rows + 8 * t).astype(F32), current[t])
                for t in range(2)
            ]
            apply_last(which, base - 16, gone, before)
            solved = panel_solve(tiles, cols, rows)
            joined = jnp.concatenate(solved, axis=0)
            high, low = split2(joined)
            high_ref[which, gone, :] = jnp.zeros((16, RANK), BF16)
            low_ref[which, gone, :] = jnp.zeros((16, RANK), BF16)
            at = pl.ds(pl.multiple_of(base, 16), 16)
            high_ref[which, at, :] = high
            low_ref[which, at, :] = low
            upcoming = []
            for t in range(2):
                tile = work_ref[which, pl.ds(pl.multiple_of(following + 8 * t, 8), 8), :]
                fresh = jnp.where(inside, 0.0, tile)
                for j in range(16):
                    weight = jnp.take_along_axis(tile, picks[j], axis=1)
                    fresh = fresh - weight * row_of(solved[j // 8], j % 8)
                upcoming.append(fresh)
            after.append((tuple(upcoming), tuple(solved)))
        return tuple(after)

    start = []
    for which in range(count):
        high_ref[which] = jnp.zeros((RANK, RANK), BF16)
        low_ref[which] = jnp.zeros((RANK, RANK), BF16)
        first = (work_ref[which, :8, :], work_ref[which, 8:16, :])
        end = (work_ref[which, 112:120, :], work_ref[which, 120:128, :])
        start.append((first, end))
    done = lax.fori_loop(0, RANK // 16, step, tuple(start))
    for which in range(count):
        apply_last(which, RANK - 16, slice(RANK - 16, RANK), done[which][1])


def part(buf_ref, index, slab):
    start = (index % 2) * 2
    return buf_ref[start : start + 2, :, index // 2, slab].reshape(RANK, RANK)


def capacitance(factor, grams):
    top = mm_exact_right(grams[0], factor[:RANK])
    low = mm_exact_right(grams[1], factor[RANK:])
    return mm_exact_left(factor, jnp.concatenate((top, low), axis=0), TN)


def identity():
    down = lax.broadcasted_iota(jnp.int32, (RANK, RANK), 0)
    return (down == lax.broadcasted_iota(jnp.int32, (RANK, RANK), 1)).astype(F32)


def finish_solve(cap, term, work_ref, high_ref, low_ref):
    inverse = work_ref[0]
    cross = cap[:RANK, RANK:]
    wide = mm(inverse, cross)
    work_ref[0] = cap[RANK:, RANK:] + identity() - mm(cross, wide, TN)
    first = mm(inverse, term[:RANK])
    rest = term[RANK:] - mm(cross, first, TN)
    invert_in_place(work_ref, high_ref, low_ref, 1)
    low = mm(work_ref[0], rest)
    top = first - mm(wide, low)
    return top, low


def vmem():
    return pl.BlockSpec(memory_space=pltpu.VMEM)


def shape(*dims, kind=F32):
    return jax.ShapeDtypeStruct(dims, kind)


def inverse_scratch():
    return [
        pltpu.VMEM((1, RANK, RANK), F32),
        pltpu.VMEM((1, RANK, RANK), BF16),
        pltpu.VMEM((1, RANK, RANK), BF16),
    ]


def body(right_side, leaf_inverse, basis_one, basis_two, factor_one, factor_two):
    rows = leaf_inverse.shape[0]
    dma = pltpu.SemaphoreType.DMA
    plane = NZ * NX - 1
    hbm = pl.BlockSpec(memory_space=pltpu.HBM)
    return pl.pallas_call(
        whole_kernel,
        out_shape=shape(64, rows),
        in_specs=[hbm] * 6,
        out_specs=vmem(),
        scratch_shapes=[
            pltpu.VMEM((rows, 2 * RANK), BF16),
            pltpu.VMEM((rows, 2 * RANK), BF16),
            pltpu.VMEM((64, rows), F32),
            pltpu.VMEM((2, RANK, 192), F32),
            pltpu.VMEM((2, 2 * RANK, 192), F32),
            pltpu.VMEM((64, rows), F32),
            pltpu.VMEM((rows, rows), F32),
            pltpu.VMEM((rows, RANK), F32),
            pltpu.VMEM((rows, RANK), F32),
            pltpu.VMEM((NX, NZ, 2, 2, 8, RANK), F32),
            pltpu.VMEM((2, NX, NZ, 8, RANK), F32),
            pltpu.VMEM((NX, NZ, 8, RANK), F32),
            pltpu.VMEM((NZ, NX, 8, RANK), F32),
            pltpu.VMEM((plane, 8, RANK), F32),
            pltpu.VMEM((8, RANK), F32),
            pltpu.VMEM((NY, 8, RANK), F32),
            pltpu.VMEM((2, 8, RANK), F32),
        ] + inverse_scratch() + [
            pltpu.VMEM(factor_one.shape, BF16),
            pltpu.VMEM(factor_two.shape, BF16),
            dma((6,)), dma, dma, dma((plane,)), dma((plane,)), dma((7,)), dma((7,)),
            dma, dma, dma((7,)), dma((7,)), dma((6,)), dma((6,)), dma((2,)), dma((2,)),
        ],
        compiler_params=pltpu.CompilerParams(
            collective_id=0, has_side_effects=True, vmem_limit_bytes=62 << 20
        ),
    )(right_side.T, leaf_inverse, basis_one, basis_two, factor_one, factor_two).T


def solution(mesh):
    split = P(("gx", "gy"), None)
    return jax.shard_map(
        body, mesh=mesh, in_specs=(split, split, split, split, P(), P()),
        out_specs=split, check_vma=False,
    )
```

time: 67.6 us -> 64 us (0.947)
  Pallas kernels: 66.3 us -> 62.2 us
    pallas_call x4 -> x1, Pallas kernels: 66.3 us -> 62.2 us  [body(): pl.pallas_call(whole_kernel, out_shape=shape(64, rows), in_specs=[hbm] *...]
    unnamed x12 -> x1, local copies, waits for them, and re-layouts: 1.06 us -> 1.57 us
where the time goes in v3:
time: 64 us; the launch traced here: 63.8 us
  Pallas kernels  62.2 us (97%)
  local copies, waits for them, and re-layouts  1.57 us (2%)
    pallas_call x1, Pallas kernels, body(): pl.pallas_call(whole_kernel, out_shape=shape(64, rows), in_specs=[hbm] *...  62.2 us
    unnamed x1, local copies, waits for them, and re-layouts  1.57 us

profile of v3, /device:TPU:1, one launch (start us, length us, event | category | flops | bytes accessed | tf_op | source)
XLA Modules:
  0.0 63.8 jit_solution(12255266195592827165)
XLA Ops:
  0.0 62.2 %shard_map.64 = f32[64,512]{1,0:T(8,128)} custom-call(f32[64,512]{1,0:T(8,128)} %bitcast.3, f32[512,512]{1,0:T(8,128)} %inv_hbm.1, f32[512,128]{1,0:T(8,128)} %one_hbm.1, f32[512,128]{1,0:T(8,128)} %two_hbm.1, bf16[1,256,256]{2,1,0:T(8,128)(2,1)} %coarse_hbm.1, bf16[2,256,256]{2,1,0:T(8,128)(2,1)} %fine_hbm.1), custom_call_target="tpu_custom_call" | custom-call | tf_op jit(solution)/shard_map/pallas_call | solution.py:399
  62.2 1.6 %copy.8 = f32[512,64]{0,1:T(8,128)} copy(f32[512,64]{0,1:T(8,128)} %bitcast.2) | data formatting | bytes 262144

commit v4 on v3

--- a/solution.py
+++ b/solution.py
@@ -90,7 +90,7 @@
     s_high_ref, s_low_ref, x_ref, schur_ref, coef_ref,
     rhs_ref, inv_ref, one_ref, two_ref, buf_ref,
     prod_ref, from_core, chip_sum, from_plane, x_sum, by_y, leaving,
-    work_ref, high_ref, low_ref, coarse_ref, fine_ref,
+    work_ref, high_ref, low_ref, coarse_ref, fine_ref, coarse_t, fine_t,
     in_s, core_s, core_r, p_s, p_r, y_s, y_r, w_s, w_r, gz_s, gz_r, gx_s, gx_r, o_s, o_r,
 ):
     gx, gy = lax.axis_index("gx"), lax.axis_index("gy")
@@ -116,13 +116,6 @@
     def y_peer(step):
         there = lax.rem(y + step, NY)
         return there, (there * 2 + x_hi, gy)
-
-    barrier = pltpu.get_barrier_semaphore()
-    peers = [plane_peer(up, over)[2] for up, over in plane_steps()]
-    peers += [y_peer(step)[1] for step in farthest_first(NY)]
-    peers += [sibling]
-    for peer in peers:
-        pl.semaphore_signal(barrier, inc=1, device_id=peer, device_id_type=MESH)
 
     loads = [
         pltpu.make_async_copy(source, target, in_s.at[index])
@@ -133,6 +126,14 @@
     ]
     for load in loads:
         load.start()
+
+    barrier = pltpu.get_barrier_semaphore()
+    peers = [plane_peer(up, over)[2] for up, over in plane_steps()]
+    peers += [y_peer(step)[1] for step in farthest_first(NY)]
+    peers += [sibling]
+    for peer in peers:
+        pl.semaphore_signal(barrier, inc=1, device_id=peer, device_id_type=MESH)
+
     for load in loads[:4]:
         load.wait()
     local_products(
@@ -161,6 +162,10 @@
         copies.append(
             send(chip_sum.at[z_there, x_there], from_plane.at[at], p_s.at[at], p_r.at[at], peer)
         )
+    for load in loads[4:]:
+        load.wait()
+    fine_t[...] = fine_ref[core].T
+    coarse_t[...] = coarse_ref[0].T
     total = chip_sum[z, x]
     for copy in copies:
         copy.wait()
@@ -201,12 +206,10 @@
     for copy in waves[0]:
         copy.wait()
 
-    for load in loads[4:]:
-        load.wait()
-    factor = fine_ref[core]
-    cap = capacitance(factor, [part(buf_ref, 0, 0), part(buf_ref, 0, 1)])
+    factor, factor_t = fine_ref[core], fine_t[...]
+    cap = capacitance(factor, factor_t, [part(buf_ref, 0, 0), part(buf_ref, 0, 1)])
     mixed = jnp.concatenate((part(buf_ref, 1, 0), part(buf_ref, 1, 1)), axis=0)
-    coarse_term = mm_exact_left(factor, mixed, TN)
+    coarse_term = mm_exact_left(factor_t, mixed)
     eye = identity()
     work_ref[0] = cap[:RANK, :RANK] + eye
     invert_in_place(work_ref, high_ref, low_ref, 1)
@@ -214,11 +217,10 @@
         copy.wait()
     rights = [part(buf_ref, 3, slab) for slab in range(2)]
     right = jnp.concatenate([rights[slab][:64].T for slab in range(2)], axis=0)
-    term = jnp.concatenate((coarse_term, mm_exact_left(factor, right, TN)), axis=1)
+    term = jnp.concatenate((coarse_term, mm_exact_left(factor_t, right)), axis=1)
     top, low = finish_solve(cap, term, work_ref, high_ref, low_ref)
     inner = mm(term[:RANK, :RANK], top, TN) + mm(term[RANK:, :RANK], low, TN)
-    coef_ref[core, :RANK] = top
-    coef_ref[core, RANK:] = low
+    coef_ref[core] = mm_exact_left(factor, jnp.concatenate((top, low), axis=0))
     schur_ref[core, :, :RANK] = part(buf_ref, 2, 0) + part(buf_ref, 2, 1) - inner[:, :RANK]
     schur_ref[core, :, RANK:] = (rights[0][64:] + rights[1][64:]).T - inner[:, RANK:]
     swaps = [
@@ -231,19 +233,18 @@
     block = lax.div(gx, 4)
     my_pair, my_half = lax.div(block, 2), lax.rem(block, 2)
     factor = coarse_ref[0]
-    cap = capacitance(factor, [schur_ref[0, :, :RANK], schur_ref[1, :, :RANK]])
+    factor_t = coarse_t[...]
+    cap = capacitance(factor, factor_t, [schur_ref[0, :, :RANK], schur_ref[1, :, :RANK]])
     term = mm_exact_left(
-        factor, jnp.concatenate((schur_ref[0, :, RANK:], schur_ref[1, :, RANK:]), axis=0), TN
+        factor_t, jnp.concatenate((schur_ref[0, :, RANK:], schur_ref[1, :, RANK:]), axis=0)
     )
     work_ref[0] = cap[:RANK, :RANK] + identity()
     invert_in_place(work_ref, high_ref, low_ref, 1)
     top, low = finish_solve(cap, term, work_ref, high_ref, low_ref)
     half_rows = pl.ds(pl.multiple_of(my_pair * RANK, RANK), RANK)
     m1 = mm_exact_left(coarse_ref[0, half_rows, :], jnp.concatenate((top, low), axis=0))
-    own = coef_ref[my_pair]
-    inner = own[:, RANK:] - mm(own[:, :RANK], m1)
-    block_rows = pl.ds(pl.multiple_of(my_half * RANK, RANK), RANK)
-    m2 = mm_exact_left(fine_ref[my_pair, block_rows, :], inner)
+    own = coef_ref[my_pair, pl.ds(pl.multiple_of(my_half * RANK, RANK), RANK), :]
+    m2 = own[:, RANK:] - mm(own[:, :RANK], m1)
     weights = jnp.concatenate((m2, m1), axis=0).T
     w_high, w_low = split2(weights)
     s_high = s_high_ref[...]
@@ -256,26 +257,38 @@
     return jnp.broadcast_to(tile[index : index + 1, :], tile.shape)
 
 
-def reciprocal(value):
-    guess = pl.reciprocal(value, approx=True)
-    guess = guess * (2.0 - value * guess)
-    return guess * (2.0 - value * guess)
-
-
-def panel_solve(tiles, cols, unit_rows):
+def spread(tile, pick):
+    column = jnp.sum(jnp.where(pick, tile, 0.0), axis=1, keepdims=True)
+    return jnp.broadcast_to(column, tile.shape)
+
+
+def combine(weights, solved):
+    sums = [jnp.zeros((8, RANK), F32)] * 4
+    for j in range(16):
+        sums[j % 4] = sums[j % 4] + weights[j] * row_of(solved[j // 8], j % 8)
+    return (sums[0] + sums[1]) + (sums[2] + sums[3])
+
+
+def panel_solve(tiles, cols, rows):
     scale = [jnp.ones((8, RANK), F32)] * 2
     cols = [list(pair) for pair in cols]
     for k in range(16):
         at, sub = k // 8, k % 8
-        inverse = reciprocal(row_of(cols[k][at], sub))
-        here = unit_rows == sub
+        pivot = row_of(cols[k][at], sub)
+        guess = pl.reciprocal(pivot, approx=True)
+        refine = 2.0 - pivot * guess
+        inverse = guess * refine
+        here = rows == sub
         scale[at] = jnp.where(here, inverse, scale[at])
-        factors = list(cols[k])
-        factors[at] = jnp.where(here, 0.0, factors[at])
-        factors = [factor * inverse for factor in factors]
+        raw = list(cols[k])
+        raw[at] = jnp.where(here, 0.0, raw[at])
+        factors = [value * inverse for value in raw]
         for j in range(k + 1, 16):
             across = row_of(cols[j][at], sub)
-            cols[j] = [cols[j][t] - factors[t] * across for t in range(2)]
+            if j == k + 1:
+                cols[j] = [cols[j][t] - (raw[t] * across * guess) * refine for t in range(2)]
+            else:
+                cols[j] = [cols[j][t] - factors[t] * across for t in range(2)]
         across = row_of(tiles[at], sub)
         tiles = [tiles[t] - factors[t] * across for t in range(2)]
     return [tiles[t] * scale[t] for t in range(2)]
@@ -300,14 +313,21 @@
     def step(panel, carry):
         base = panel * 16
         inside = jnp.logical_and(lanes >= base, lanes < base + 16)
-        picks = [jnp.full((8, RANK), base + j, jnp.int32) for j in range(16)]
-        following = lax.rem(base + 16, RANK)
+        earlier = jnp.logical_and(lanes >= base - 16, lanes < base)
+        picks = [lanes == base + j for j in range(16)]
+        last_picks = [lanes == base - 16 + j for j in range(16)]
+        following = lax.rem(base + 32, RANK)
         gone = pl.ds(pl.multiple_of(lax.rem(base + RANK - 16, RANK), 16), 16)
         after = []
         for which in range(count):
-            current, before = carry[which]
+            current, coming, before = carry[which]
+            old = [[spread(tile, pick) for pick in last_picks] for tile in coming]
+            coming = [
+                jnp.where(earlier, 0.0, coming[t]) - combine(old[t], before) for t in range(2)
+            ]
+            weights = [[spread(tile, pick) for pick in picks] for tile in coming]
             cols = [
-                [jnp.take_along_axis(current[t], picks[j], axis=1) for t in range(2)]
+                [spread(current[t], picks[j]) for t in range(2)]
                 for j in range(16)
             ]
             tiles = [
@@ -323,15 +343,13 @@
             at = pl.ds(pl.multiple_of(base, 16), 16)
             high_ref[which, at, :] = high
             low_ref[which, at, :] = low
-            upcoming = []
-            for t in range(2):
-                tile = work_ref[which, pl.ds(pl.multiple_of(following + 8 * t, 8), 8), :]
-                fresh = jnp.where(inside, 0.0, tile)
-                for j in range(16):
-                    weight = jnp.take_along_axis(tile, picks[j], axis=1)
-                    fresh = fresh - weight * row_of(solved[j // 8], j % 8)
-                upcoming.append(fresh)
-            after.append((tuple(upcoming), tuple(solved)))
+            upcoming = [
+                jnp.where(inside, 0.0, coming[t]) - combine(weights[t], solved) for t in range(2)
+            ]
+            stale = [
+                work_ref[which, pl.ds(pl.multiple_of(following + 8 * t, 8), 8), :] for t in range(2)
+            ]
+            after.append((tuple(upcoming), tuple(stale), tuple(solved)))
         return tuple(after)
 
     start = []
@@ -340,10 +358,11 @@
         low_ref[which] = jnp.zeros((RANK, RANK), BF16)
         first = (work_ref[which, :8, :], work_ref[which, 8:16, :])
         end = (work_ref[which, 112:120, :], work_ref[which, 120:128, :])
-        start.append((first, end))
+        second = (work_ref[which, 16:24, :], work_ref[which, 24:32, :])
+        start.append((first, second, end))
     done = lax.fori_loop(0, RANK // 16, step, tuple(start))
     for which in range(count):
-        apply_last(which, RANK - 16, slice(RANK - 16, RANK), done[which][1])
+        apply_last(which, RANK - 16, slice(RANK - 16, RANK), done[which][2])
 
 
 def part(buf_ref, index, slab):
@@ -351,10 +370,10 @@
     return buf_ref[start : start + 2, :, index // 2, slab].reshape(RANK, RANK)
 
 
-def capacitance(factor, grams):
+def capacitance(factor, factor_t, grams):
     top = mm_exact_right(grams[0], factor[:RANK])
     low = mm_exact_right(grams[1], factor[RANK:])
-    return mm_exact_left(factor, jnp.concatenate((top, low), axis=0), TN)
+    return mm_exact_left(factor_t, jnp.concatenate((top, low), axis=0))
 
 
 def identity():
@@ -364,11 +383,11 @@
 
 def finish_solve(cap, term, work_ref, high_ref, low_ref):
     inverse = work_ref[0]
-    cross = cap[:RANK, RANK:]
-    wide = mm(inverse, cross)
-    work_ref[0] = cap[RANK:, RANK:] + identity() - mm(cross, wide, TN)
+    wide = mm(inverse, cap[:RANK, RANK:])
+    cross = cap[RANK:, :RANK]
+    work_ref[0] = cap[RANK:, RANK:] + identity() - mm(cross, wide)
     first = mm(inverse, term[:RANK])
-    rest = term[RANK:] - mm(cross, first, TN)
+    rest = term[RANK:] - mm(cross, first)
     invert_in_place(work_ref, high_ref, low_ref, 1)
     low = mm(work_ref[0], rest)
     top = first - mm(wide, low)
@@ -422,6 +441,8 @@
         ] + inverse_scratch() + [
             pltpu.VMEM(factor_one.shape, BF16),
             pltpu.VMEM(factor_two.shape, BF16),
+            pltpu.VMEM((2 * RANK, 2 * RANK), BF16),
+            pltpu.VMEM((2 * RANK, 2 * RANK), BF16),
             dma((6,)), dma, dma, dma((plane,)), dma((plane,)), dma((7,)), dma((7,)),
             dma, dma, dma((7,)), dma((7,)), dma((6,)), dma((6,)), dma((2,)), dma((2,)),
         ],

time: 64 us -> 61.8 us (0.966)
  Pallas kernels: 62.2 us -> 60.1 us
    pallas_call x1, Pallas kernels: 62.2 us -> 60.1 us  [body(): pl.pallas_call(whole_kernel, out_shape=shape(64, rows), in_specs=[hbm] *...]
where the time goes in v4:
time: 61.8 us; the launch traced here: 61.7 us
  Pallas kernels  60.1 us (97%)
  local copies, waits for them, and re-layouts  1.57 us (3%)
    pallas_call x1, Pallas kernels, body(): pl.pallas_call(whole_kernel, out_shape=shape(64, rows), in_specs=[hbm] *...  60.1 us
    unnamed x1, local copies, waits for them, and re-layouts  1.57 us

profile of v4, /device:TPU:1, one launch (start us, length us, event | category | flops | bytes accessed | tf_op | source)
XLA Modules:
  0.0 61.7 jit_solution(9455611935249039476)
XLA Ops:
  0.0 60.1 %shard_map.64 = f32[64,512]{1,0:T(8,128)} custom-call(f32[64,512]{1,0:T(8,128)} %bitcast.3, f32[512,512]{1,0:T(8,128)} %inv_hbm.1, f32[512,128]{1,0:T(8,128)} %one_hbm.1, f32[512,128]{1,0:T(8,128)} %two_hbm.1, bf16[1,256,256]{2,1,0:T(8,128)(2,1)} %coarse_hbm.1, bf16[2,256,256]{2,1,0:T(8,128)(2,1)} %fine_hbm.1), custom_call_target="tpu_custom_call" | custom-call | tf_op jit(solution)/shard_map/pallas_call | solution.py:418
  60.1 1.6 %copy.8 = f32[512,64]{0,1:T(8,128)} copy(f32[512,64]{0,1:T(8,128)} %bitcast.2) | data formatting | bytes 262144

commit v5 on v4

--- a/solution.py
+++ b/solution.py
@@ -74,12 +74,12 @@
     grams = dot(both_high, s_high, TN) + (dot(both_high, s_low, TN) + dot(both_low, s_high, TN))
     x_high, x_low = split2(x_t)
     projs = dot(x_high, both_high, NN) + (dot(x_high, both_low, NN) + dot(x_low, both_high, NN))
-    shape = (2, NZ, 8, RANK)
-    prod_ref[0, 0:2] = grams[:RANK, :RANK].reshape(shape)
-    prod_ref[0, 2:4] = grams[:RANK, RANK:].reshape(shape)
-    prod_ref[1, 0:2] = grams[RANK:, RANK:].reshape(shape)
-    prod_ref[1, 2] = projs[:, :RANK].reshape(shape[1:])
-    prod_ref[1, 3] = projs[:, RANK:].reshape(shape[1:])
+    shape = (NX, NZ // 2, 8, RANK)
+    prod_ref[0, :, :4] = grams[:RANK, :RANK].reshape(shape)
+    prod_ref[0, :, 4:] = grams[:RANK, RANK:].reshape(shape)
+    prod_ref[1, :, :4] = grams[RANK:, RANK:].reshape(shape)
+    prod_ref[1, :2, 4:] = projs[:, :RANK].reshape(2, NZ // 2, 8, RANK)
+    prod_ref[1, 2:, 4:] = projs[:, RANK:].reshape(2, NZ // 2, 8, RANK)
     s_high_ref[...] = s_high
     s_low_ref[...] = s_low
     x_ref[...] = x_t
@@ -89,15 +89,15 @@
     rhs_hbm, inv_hbm, one_hbm, two_hbm, coarse_hbm, fine_hbm, out_ref,
     s_high_ref, s_low_ref, x_ref, schur_ref, coef_ref,
     rhs_ref, inv_ref, one_ref, two_ref, buf_ref,
-    prod_ref, from_core, chip_sum, from_plane, x_sum, by_y, leaving,
+    prod_ref, from_core, chip_sum, from_plane, x_sum, by_y,
     work_ref, high_ref, low_ref, coarse_ref, fine_ref, coarse_t, fine_t,
-    in_s, core_s, core_r, p_s, p_r, y_s, y_r, w_s, w_r, gz_s, gz_r, gx_s, gx_r, o_s, o_r,
+    in_s, core_s, core_r, p_s, p_r, y_s, y_r, gz_s, gz_r, gx_s, gx_r, o_s, o_r,
 ):
     gx, gy = lax.axis_index("gx"), lax.axis_index("gy")
     y, x_hi = lax.div(gx, 2), lax.rem(gx, 2)
     z, x_lo, core = lax.div(gy, 4), lax.rem(lax.div(gy, 2), 2), lax.rem(gy, 2)
     x = x_hi * 2 + x_lo
-    other = 1 - core
+    other, solver = 1 - core, lax.div(y, 4)
     sibling = (gx, gy + 1 - 2 * core)
 
     def plane_peer(up, over):
@@ -112,10 +112,6 @@
     def x_peer(step):
         there = lax.rem(x + step, NX)
         return there, (y * 2 + lax.div(there, 2), z * 4 + lax.rem(there, 2) * 2 + core)
-
-    def y_peer(step):
-        there = lax.rem(y + step, NY)
-        return there, (there * 2 + x_hi, gy)
 
     loads = [
         pltpu.make_async_copy(source, target, in_s.at[index])
@@ -129,7 +125,10 @@
 
     barrier = pltpu.get_barrier_semaphore()
     peers = [plane_peer(up, over)[2] for up, over in plane_steps()]
-    peers += [y_peer(step)[1] for step in farthest_first(NY)]
+    for step in farthest_first(NY):
+        there = lax.rem(y + step, NY)
+        for which in range(2):
+            peers.append((there * 2 + x_hi, z * 4 + x_lo * 2 + which))
     peers += [sibling]
     for peer in peers:
         pl.semaphore_signal(barrier, inc=1, device_id=peer, device_id_type=MESH)
@@ -174,17 +173,34 @@
     x_sum[...] = total
 
     copies = []
+    own = lax.rem(y, 4) * 2 + core
+    slot = by_y.at[lax.rem(y, 4), core]
     for step in farthest_first(NY):
-        _, peer = y_peer(step)
-        copies.append(send(x_sum, by_y.at[y], y_s.at[step - 1], y_r.at[step - 1], peer))
-    by_y[y] = total
+        there = lax.rem(y + step, NY)
+        peer = (there * 2 + x_hi, z * 4 + x_lo * 2 + solver)
+        copies.append(send(x_sum, slot, y_s.at[step - 1], y_r.at[own], peer))
+
+    @pl.when(solver == core)
+    def _():
+        by_y[lax.rem(y, 4), core] = total
+
+    @pl.when(solver != core)
+    def _():
+        send(x_sum, slot, y_s.at[7], y_r.at[own], sibling).wait_send()
+
     for copy in copies:
-        copy.wait()
-    for slab in range(2):
-        here, there = core * 4 + 2 * slab, other * 4 + 2 * slab
-        leaving[slab] = by_y[there] + by_y[there + 1]
-        buf_ref[x, z, core, slab] = by_y[here] + by_y[here + 1]
-    send(leaving, buf_ref.at[x, z, core], w_s, w_r, sibling).wait()
+        copy.wait_send()
+    for at in range(8):
+        @pl.when(jnp.logical_not(jnp.logical_and(solver == core, own == at)))
+        def _():
+            pltpu.make_async_remote_copy(
+                src_ref=x_sum, dst_ref=by_y.at[at // 2, at % 2], send_sem=y_s.at[0],
+                recv_sem=y_r.at[at], device_id=sibling, device_id_type=MESH,
+            ).wait_recv()
+
+    for half in range(2):
+        for slab in range(2):
+            buf_ref[x, z, half, slab] = by_y[2 * slab, half] + by_y[2 * slab + 1, half]
 
     copies = []
     place = buf_ref.at[x, z]
@@ -195,8 +211,8 @@
         copy.wait()
 
     waves = []
-    for wave in range(2):
-        place = buf_ref.at[x, :, wave]
+    for wave, (first_z, count_z, half) in enumerate(((0, 4, 0), (4, 4, 0), (0, NZ, 1))):
+        place = buf_ref.at[x, pl.ds(first_z, count_z), half]
         copies = []
         for step in farthest_first(NX):
             _, peer = x_peer(step)
@@ -208,13 +224,13 @@
 
     factor, factor_t = fine_ref[core], fine_t[...]
     cap = capacitance(factor, factor_t, [part(buf_ref, 0, 0), part(buf_ref, 0, 1)])
-    mixed = jnp.concatenate((part(buf_ref, 1, 0), part(buf_ref, 1, 1)), axis=0)
-    coarse_term = mm_exact_left(factor_t, mixed)
     eye = identity()
     work_ref[0] = cap[:RANK, :RANK] + eye
     invert_in_place(work_ref, high_ref, low_ref, 1)
-    for copy in waves[1]:
+    for copy in waves[1] + waves[2]:
         copy.wait()
+    mixed = jnp.concatenate((part(buf_ref, 1, 0), part(buf_ref, 1, 1)), axis=0)
+    coarse_term = mm_exact_left(factor_t, mixed)
     rights = [part(buf_ref, 3, slab) for slab in range(2)]
     right = jnp.concatenate([rights[slab][:64].T for slab in range(2)], axis=0)
     term = jnp.concatenate((coarse_term, mm_exact_left(factor_t, right)), axis=1)
@@ -366,8 +382,8 @@
 
 
 def part(buf_ref, index, slab):
-    start = (index % 2) * 2
-    return buf_ref[start : start + 2, :, index // 2, slab].reshape(RANK, RANK)
+    start = (index % 2) * 4
+    return buf_ref[:, start : start + 4, index // 2, slab].reshape(RANK, RANK)
 
 
 def capacitance(factor, factor_t, grams):
@@ -436,18 +452,17 @@
             pltpu.VMEM((NZ, NX, 8, RANK), F32),
             pltpu.VMEM((plane, 8, RANK), F32),
             pltpu.VMEM((8, RANK), F32),
-            pltpu.VMEM((NY, 8, RANK), F32),
-            pltpu.VMEM((2, 8, RANK), F32),
+            pltpu.VMEM((4, 2, 8, RANK), F32),
         ] + inverse_scratch() + [
             pltpu.VMEM(factor_one.shape, BF16),
             pltpu.VMEM(factor_two.shape, BF16),
             pltpu.VMEM((2 * RANK, 2 * RANK), BF16),
             pltpu.VMEM((2 * RANK, 2 * RANK), BF16),
-            dma((6,)), dma, dma, dma((plane,)), dma((plane,)), dma((7,)), dma((7,)),
-            dma, dma, dma((7,)), dma((7,)), dma((6,)), dma((6,)), dma((2,)), dma((2,)),
+            dma((6,)), dma, dma, dma((plane,)), dma((plane,)), dma((8,)), dma((8,)),
+            dma((7,)), dma((7,)), dma((9,)), dma((9,)), dma((2,)), dma((2,)),
         ],
         compiler_params=pltpu.CompilerParams(
-            collective_id=0, has_side_effects=True, vmem_limit_bytes=62 << 20
+            collective_id=0, has_side_effects=True, vmem_limit_bytes=56_400_000
         ),
     )(right_side.T, leaf_inverse, basis_one, basis_two, factor_one, factor_two).T
 

time: 61.8 us -> 55.8 us (0.903)
  Pallas kernels: 60.1 us -> 55 us
  local copies, waits for them, and re-layouts: 1.57 us -> 0.66 us
    pallas_call x1, Pallas kernels: 60.1 us -> 55 us  [body(): pl.pallas_call(whole_kernel, out_shape=shape(64, rows), in_specs=[hbm] *...]
    unnamed x1, local copies, waits for them, and re-layouts: 1.57 us -> 0.66 us
where the time goes in v5:
time: 55.8 us; the launch traced here: 55.7 us
  Pallas kernels  55 us (99%)
  local copies, waits for them, and re-layouts  0.66 us (1%)
    pallas_call x1, Pallas kernels, body(): pl.pallas_call(whole_kernel, out_shape=shape(64, rows), in_specs=[hbm] *...  55 us

profile of v5, /device:TPU:1, one launch (start us, length us, event | category | flops | bytes accessed | tf_op | source)
XLA Modules:
  0.0 55.7 jit_solution(15131600318026005552)
XLA Ops:
  0.0 55.0 %shard_map.64 = f32[64,512]{1,0:T(8,128)S(1)} custom-call(f32[64,512]{1,0:T(8,128)} %bitcast.3, f32[512,512]{1,0:T(8,128)} %inv_hbm.1, f32[512,128]{1,0:T(8,128)} %one_hbm.1, f32[512,128]{1,0:T(8,128)} %two_hbm.1, bf16[1,256,256]{2,1,0:T(8,128)(2,1)} %coarse_hbm.1, bf16[2,256,256]{2,1,0:T(8,128)(2,1)} %fine_hbm.1), custom_call_target="tpu_custom_call" | custom-call | tf_op jit(solution)/shard_map/pallas_call | solution.py:434
  55.0 0.7 %copy.8 = f32[512,64]{0,1:T(8,128)} copy(f32[512,64]{0,1:T(8,128)S(1)} %bitcast.2) | data formatting | bytes 262144

commit v6 on v5

--- a/solution.py
+++ b/solution.py
@@ -234,17 +234,19 @@
     rights = [part(buf_ref, 3, slab) for slab in range(2)]
     right = jnp.concatenate([rights[slab][:64].T for slab in range(2)], axis=0)
     term = jnp.concatenate((coarse_term, mm_exact_left(factor_t, right)), axis=1)
-    top, low = finish_solve(cap, term, work_ref, high_ref, low_ref)
-    inner = mm(term[:RANK, :RANK], top, TN) + mm(term[RANK:, :RANK], low, TN)
-    coef_ref[core] = mm_exact_left(factor, jnp.concatenate((top, low), axis=0))
+    wide, first, rest = eliminate(cap, term, work_ref)
+    inner = mm(term[:RANK, :RANK], first, TN)
+    rest_t = rest[:, :RANK].T
+    invert_in_place(work_ref, high_ref, low_ref, 1)
+    low = mm(work_ref[0], rest)
+    inner = inner + mm(rest_t, low)
     schur_ref[core, :, :RANK] = part(buf_ref, 2, 0) + part(buf_ref, 2, 1) - inner[:, :RANK]
     schur_ref[core, :, RANK:] = (rights[0][64:] + rights[1][64:]).T - inner[:, RANK:]
-    swaps = [
-        send(ref.at[core], ref.at[core], o_s.at[at], o_r.at[at], sibling)
-        for at, ref in enumerate((schur_ref, coef_ref))
-    ]
-    for swap in swaps:
-        swap.wait()
+    schur_swap = send(schur_ref.at[core], schur_ref.at[core], o_s.at[0], o_r.at[0], sibling)
+    top = first - mm(wide, low)
+    coef_ref[core] = mm_exact_left(factor, jnp.concatenate((top, low), axis=0))
+    coef_swap = send(coef_ref.at[core], coef_ref.at[core], o_s.at[1], o_r.at[1], sibling)
+    schur_swap.wait()
 
     block = lax.div(gx, 4)
     my_pair, my_half = lax.div(block, 2), lax.rem(block, 2)
@@ -256,9 +258,14 @@
     )
     work_ref[0] = cap[:RANK, :RANK] + identity()
     invert_in_place(work_ref, high_ref, low_ref, 1)
-    top, low = finish_solve(cap, term, work_ref, high_ref, low_ref)
-    half_rows = pl.ds(pl.multiple_of(my_pair * RANK, RANK), RANK)
-    m1 = mm_exact_left(coarse_ref[0, half_rows, :], jnp.concatenate((top, low), axis=0))
+    wide, first, rest = eliminate(cap, term, work_ref)
+    my_factor = coarse_ref[0, pl.ds(pl.multiple_of(my_pair * RANK, RANK), RANK), :]
+    fixed = mm_exact_left(my_factor[:, :RANK], first)
+    spare = my_factor[:, RANK:].astype(F32) - mm_exact_left(my_factor[:, :RANK], wide)
+    invert_in_place(work_ref, high_ref, low_ref, 1)
+    low = mm(work_ref[0], rest)
+    m1 = fixed + mm(spare, low)
+    coef_swap.wait()
     own = coef_ref[my_pair, pl.ds(pl.multiple_of(my_half * RANK, RANK), RANK), :]
     m2 = own[:, RANK:] - mm(own[:, :RANK], m1)
     weights = jnp.concatenate((m2, m1), axis=0).T
@@ -397,17 +404,14 @@
     return (down == lax.broadcasted_iota(jnp.int32, (RANK, RANK), 1)).astype(F32)
 
 
-def finish_solve(cap, term, work_ref, high_ref, low_ref):
+def eliminate(cap, term, work_ref):
     inverse = work_ref[0]
     wide = mm(inverse, cap[:RANK, RANK:])
     cross = cap[RANK:, :RANK]
     work_ref[0] = cap[RANK:, RANK:] + identity() - mm(cross, wide)
     first = mm(inverse, term[:RANK])
     rest = term[RANK:] - mm(cross, first)
-    invert_in_place(work_ref, high_ref, low_ref, 1)
-    low = mm(work_ref[0], rest)
-    top = first - mm(wide, low)
-    return top, low
+    return wide, first, rest
 
 
 def vmem():

time: 55.8 us -> 55.2 us (0.989)
  Pallas kernels: 55 us -> 54.3 us
    pallas_call x1, Pallas kernels: 55 us -> 54.3 us  [body(): pl.pallas_call(whole_kernel, out_shape=shape(64, rows), in_specs=[hbm] *...]
where the time goes in v6:
time: 55.2 us; the launch traced here: 55 us
  Pallas kernels  54.3 us (98%)
  local copies, waits for them, and re-layouts  0.66 us (1%)
    pallas_call x1, Pallas kernels, body(): pl.pallas_call(whole_kernel, out_shape=shape(64, rows), in_specs=[hbm] *...  54.3 us

profile of v6, /device:TPU:1, one launch (start us, length us, event | category | flops | bytes accessed | tf_op | source)
XLA Modules:
  0.0 55.0 jit_solution(7686415099795241864)
XLA Ops:
  0.0 54.3 %shard_map.64 = f32[64,512]{1,0:T(8,128)S(1)} custom-call(f32[64,512]{1,0:T(8,128)} %bitcast.3, f32[512,512]{1,0:T(8,128)} %inv_hbm.1, f32[512,128]{1,0:T(8,128)} %one_hbm.1, f32[512,128]{1,0:T(8,128)} %two_hbm.1, bf16[1,256,256]{2,1,0:T(8,128)(2,1)} %coarse_hbm.1, bf16[2,256,256]{2,1,0:T(8,128)(2,1)} %fine_hbm.1), custom_call_target="tpu_custom_call" | custom-call | tf_op jit(solution)/shard_map/pallas_call | solution.py:438
  54.4 0.7 %copy.8 = f32[512,64]{0,1:T(8,128)} copy(f32[512,64]{0,1:T(8,128)S(1)} %bitcast.2) | data formatting | bytes 262144

commit v7 on v6

--- a/solution.py
+++ b/solution.py
@@ -90,7 +90,7 @@
     s_high_ref, s_low_ref, x_ref, schur_ref, coef_ref,
     rhs_ref, inv_ref, one_ref, two_ref, buf_ref,
     prod_ref, from_core, chip_sum, from_plane, x_sum, by_y,
-    work_ref, high_ref, low_ref, coarse_ref, fine_ref, coarse_t, fine_t,
+    work_ref, high_ref, low_ref, coarse_ref, fine_ref, coarse_t, fine_t, s_high_t, s_low_t,
     in_s, core_s, core_r, p_s, p_r, y_s, y_r, gz_s, gz_r, gx_s, gx_r, o_s, o_r,
 ):
     gx, gy = lax.axis_index("gx"), lax.axis_index("gy")
@@ -164,6 +164,8 @@
     for load in loads[4:]:
         load.wait()
     fine_t[...] = fine_ref[core].T
+    s_high_t[...] = s_high_ref[...].T
+    s_low_t[...] = s_low_ref[...].T
     coarse_t[...] = coarse_ref[0].T
     total = chip_sum[z, x]
     for copy in copies:
@@ -202,16 +204,21 @@
         for slab in range(2):
             buf_ref[x, z, half, slab] = by_y[2 * slab, half] + by_y[2 * slab + 1, half]
 
-    copies = []
-    place = buf_ref.at[x, z]
-    for step in farthest_first(NZ):
-        _, peer = z_peer(step)
-        copies.append(send(place, place, gz_s.at[step - 1], gz_r.at[step - 1], peer))
-    for copy in copies:
-        copy.wait()
+    over_z = []
+    for half in range(2):
+        place = buf_ref.at[x, z, half]
+        copies = []
+        for step in farthest_first(NZ):
+            _, peer = z_peer(step)
+            at = half * 7 + step - 1
+            copies.append(send(place, place, gz_s.at[at], gz_r.at[at], peer))
+        over_z.append(copies)
 
     waves = []
     for wave, (first_z, count_z, half) in enumerate(((0, 4, 0), (4, 4, 0), (0, NZ, 1))):
+        if wave != 1:
+            for copy in over_z[half]:
+                copy.wait()
         place = buf_ref.at[x, pl.ds(first_z, count_z), half]
         copies = []
         for step in farthest_first(NX):
@@ -226,7 +233,7 @@
     cap = capacitance(factor, factor_t, [part(buf_ref, 0, 0), part(buf_ref, 0, 1)])
     eye = identity()
     work_ref[0] = cap[:RANK, :RANK] + eye
-    invert_in_place(work_ref, high_ref, low_ref, 1)
+    invert_in_place(work_ref, high_ref, low_ref)
     for copy in waves[1] + waves[2]:
         copy.wait()
     mixed = jnp.concatenate((part(buf_ref, 1, 0), part(buf_ref, 1, 1)), axis=0)
@@ -237,7 +244,7 @@
     wide, first, rest = eliminate(cap, term, work_ref)
     inner = mm(term[:RANK, :RANK], first, TN)
     rest_t = rest[:, :RANK].T
-    invert_in_place(work_ref, high_ref, low_ref, 1)
+    invert_in_place(work_ref, high_ref, low_ref)
     low = mm(work_ref[0], rest)
     inner = inner + mm(rest_t, low)
     schur_ref[core, :, :RANK] = part(buf_ref, 2, 0) + part(buf_ref, 2, 1) - inner[:, :RANK]
@@ -257,22 +264,22 @@
         factor_t, jnp.concatenate((schur_ref[0, :, RANK:], schur_ref[1, :, RANK:]), axis=0)
     )
     work_ref[0] = cap[:RANK, :RANK] + identity()
-    invert_in_place(work_ref, high_ref, low_ref, 1)
+    invert_in_place(work_ref, high_ref, low_ref)
     wide, first, rest = eliminate(cap, term, work_ref)
     my_factor = coarse_ref[0, pl.ds(pl.multiple_of(my_pair * RANK, RANK), RANK), :]
-    fixed = mm_exact_left(my_factor[:, :RANK], first)
+    fixed_t = mm_exact_left(my_factor[:, :RANK], first).T
     spare = my_factor[:, RANK:].astype(F32) - mm_exact_left(my_factor[:, :RANK], wide)
-    invert_in_place(work_ref, high_ref, low_ref, 1)
-    low = mm(work_ref[0], rest)
-    m1 = fixed + mm(spare, low)
+    spare_t, rest_t = spare.T, rest.T
     coef_swap.wait()
     own = coef_ref[my_pair, pl.ds(pl.multiple_of(my_half * RANK, RANK), RANK), :]
-    m2 = own[:, RANK:] - mm(own[:, :RANK], m1)
-    weights = jnp.concatenate((m2, m1), axis=0).T
-    w_high, w_low = split2(weights)
-    s_high = s_high_ref[...]
+    own_s_t, own_x_t = own[:, :RANK].T, own[:, RANK:].T
+    invert_in_place(work_ref, high_ref, low_ref)
+    m1_t = fixed_t + mm(mm(rest_t, work_ref[0]), spare_t)
+    m2_t = own_x_t - mm(m1_t, own_s_t)
+    w_high, w_low = split2(jnp.concatenate((m2_t, m1_t), axis=1))
+    s_high = s_high_t[...]
     out_ref[...] = x_ref[...] - (
-        dot(w_high, s_high, NT) + (dot(w_high, s_low_ref[...], NT) + dot(w_low, s_high, NT))
+        dot(w_high, s_high, NN) + (dot(w_high, s_low_t[...], NN) + dot(w_low, s_high, NN))
     )
 
 
@@ -317,75 +324,70 @@
     return [tiles[t] * scale[t] for t in range(2)]
 
 
-def invert_in_place(work_ref, high_ref, low_ref, count):
+def invert_in_place(work_ref, high_ref, low_ref, count=1):
     rows = lax.broadcasted_iota(jnp.int32, (8, RANK), 0)
     lanes = lax.broadcasted_iota(jnp.int32, (8, RANK), 1)
-    tile_count = RANK // 8
-
-    def apply_last(which, base_before, place, before):
+    ends = RANK - 16
+
+    def apply_last(base_before, place, before):
         last = jnp.logical_and(lanes >= base_before, lanes < base_before + 16)
-        whole = work_ref[which]
+        whole = work_ref[0]
         left_high, left_low = split2(whole)
-        high, low = high_ref[which], low_ref[which]
+        high, low = high_ref[0], low_ref[0]
         update = dot(left_high, high, NN) + (dot(left_high, low, NN) + dot(left_low, high, NN))
-        for tile in range(tile_count):
+        for tile in range(RANK // 8):
             at = slice(tile * 8, tile * 8 + 8)
-            work_ref[which, at, :] = jnp.where(last, 0.0, whole[at]) - update[at]
-        work_ref[which, place, :] = jnp.concatenate(before, axis=0)
+            work_ref[0, at, :] = jnp.where(last, 0.0, whole[at]) - update[at]
+        work_ref[0, place, :] = jnp.concatenate(before, axis=0)
+
+    def reduce_panel(base, current):
+        inside = jnp.logical_and(lanes >= base, lanes < base + 16)
+        picks = [lanes == base + j for j in range(16)]
+        cols = [[spread(current[t], pick) for t in range(2)] for pick in picks]
+        tiles = [
+            jnp.where(inside, (lanes - base == rows + 8 * t).astype(F32), current[t])
+            for t in range(2)
+        ]
+        return inside, picks, tiles, cols
+
+    def keep(solved, gone, at):
+        high, low = split2(jnp.concatenate(solved, axis=0))
+        high_ref[0, gone, :] = jnp.zeros((16, RANK), BF16)
+        low_ref[0, gone, :] = jnp.zeros((16, RANK), BF16)
+        high_ref[0, at, :] = high
+        low_ref[0, at, :] = low
 
     def step(panel, carry):
+        current, coming, before = carry
         base = panel * 16
-        inside = jnp.logical_and(lanes >= base, lanes < base + 16)
+        gone = pl.ds(pl.multiple_of(lax.rem(base + ends, RANK), 16), 16)
+        following = lax.rem(base + 32, RANK)
+        inside, picks, tiles, cols = reduce_panel(base, current)
         earlier = jnp.logical_and(lanes >= base - 16, lanes < base)
-        picks = [lanes == base + j for j in range(16)]
-        last_picks = [lanes == base - 16 + j for j in range(16)]
-        following = lax.rem(base + 32, RANK)
-        gone = pl.ds(pl.multiple_of(lax.rem(base + RANK - 16, RANK), 16), 16)
-        after = []
-        for which in range(count):
-            current, coming, before = carry[which]
-            old = [[spread(tile, pick) for pick in last_picks] for tile in coming]
-            coming = [
-                jnp.where(earlier, 0.0, coming[t]) - combine(old[t], before) for t in range(2)
-            ]
-            weights = [[spread(tile, pick) for pick in picks] for tile in coming]
-            cols = [
-                [spread(current[t], picks[j]) for t in range(2)]
-                for j in range(16)
-            ]
-            tiles = [
-                jnp.where(inside, (lanes - base == rows + 8 * t).astype(F32), current[t])
-                for t in range(2)
-            ]
-            apply_last(which, base - 16, gone, before)
-            solved = panel_solve(tiles, cols, rows)
-            joined = jnp.concatenate(solved, axis=0)
-            high, low = split2(joined)
-            high_ref[which, gone, :] = jnp.zeros((16, RANK), BF16)
-            low_ref[which, gone, :] = jnp.zeros((16, RANK), BF16)
-            at = pl.ds(pl.multiple_of(base, 16), 16)
-            high_ref[which, at, :] = high
-            low_ref[which, at, :] = low
-            upcoming = [
-                jnp.where(inside, 0.0, coming[t]) - combine(weights[t], solved) for t in range(2)
-            ]
-            stale = [
-                work_ref[which, pl.ds(pl.multiple_of(following + 8 * t, 8), 8), :] for t in range(2)
-            ]
-            after.append((tuple(upcoming), tuple(stale), tuple(solved)))
-        return tuple(after)
-
-    start = []
-    for which in range(count):
-        high_ref[which] = jnp.zeros((RANK, RANK), BF16)
-        low_ref[which] = jnp.zeros((RANK, RANK), BF16)
-        first = (work_ref[which, :8, :], work_ref[which, 8:16, :])
-        end = (work_ref[which, 112:120, :], work_ref[which, 120:128, :])
-        second = (work_ref[which, 16:24, :], work_ref[which, 24:32, :])
-        start.append((first, second, end))
-    done = lax.fori_loop(0, RANK // 16, step, tuple(start))
-    for which in range(count):
-        apply_last(which, RANK - 16, slice(RANK - 16, RANK), done[which][2])
+        old = [[spread(tile, lanes == base - 16 + j) for j in range(16)] for tile in coming]
+        coming = [jnp.where(earlier, 0.0, coming[t]) - combine(old[t], before) for t in range(2)]
+        weights = [[spread(tile, pick) for pick in picks] for tile in coming]
+        apply_last(base - 16, gone, before)
+        solved = panel_solve(tiles, cols, rows)
+        keep(solved, gone, pl.ds(pl.multiple_of(base, 16), 16))
+        upcoming = tuple(
+            jnp.where(inside, 0.0, coming[t]) - combine(weights[t], solved) for t in range(2)
+        )
+        stale = tuple(
+            work_ref[0, pl.ds(pl.multiple_of(following + 8 * t, 8), 8), :] for t in range(2)
+        )
+        return upcoming, stale, tuple(solved)
+
+    high_ref[0] = jnp.zeros((RANK, RANK), BF16)
+    low_ref[0] = jnp.zeros((RANK, RANK), BF16)
+    tile_at = lambda start: work_ref[0, start : start + 8, :]
+    start = ((tile_at(0), tile_at(8)), (tile_at(16), tile_at(24)), (tile_at(112), tile_at(120)))
+    current, _, before = lax.fori_loop(0, RANK // 16 - 1, step, start)
+    _, _, tiles, cols = reduce_panel(ends, current)
+    apply_last(ends - 16, slice(ends - 16, ends), before)
+    solved = panel_solve(tiles, cols, rows)
+    keep(solved, slice(ends - 16, ends), slice(ends, RANK))
+    apply_last(ends, slice(ends, RANK), solved)
 
 
 def part(buf_ref, index, slab):
@@ -462,8 +464,10 @@
             pltpu.VMEM(factor_two.shape, BF16),
             pltpu.VMEM((2 * RANK, 2 * RANK), BF16),
             pltpu.VMEM((2 * RANK, 2 * RANK), BF16),
+            pltpu.VMEM((2 * RANK, rows), BF16),
+            pltpu.VMEM((2 * RANK, rows), BF16),
             dma((6,)), dma, dma, dma((plane,)), dma((plane,)), dma((8,)), dma((8,)),
-            dma((7,)), dma((7,)), dma((9,)), dma((9,)), dma((2,)), dma((2,)),
+            dma((14,)), dma((14,)), dma((9,)), dma((9,)), dma((2,)), dma((2,)),
         ],
         compiler_params=pltpu.CompilerParams(
             collective_id=0, has_side_effects=True, vmem_limit_bytes=56_400_000

time: 55.2 us -> 55.2 us (level)
  no operation moved by 1% of the time
where the time goes in v7:
time: 55.2 us; the launch traced here: 55 us
  Pallas kernels  54.4 us (99%)
  local copies, waits for them, and re-layouts  0.66 us (1%)
    pallas_call x1, Pallas kernels, body(): pl.pallas_call(whole_kernel, out_shape=shape(64, rows), in_specs=[hbm] *...  54.4 us

profile of v7, /device:TPU:1, one launch (start us, length us, event | category | flops | bytes accessed | tf_op | source)
XLA Modules:
  0.0 55.0 jit_solution(15725519312087369145)
XLA Ops:
  0.0 54.4 %shard_map.64 = f32[64,512]{1,0:T(8,128)S(1)} custom-call(f32[64,512]{1,0:T(8,128)} %bitcast.3, f32[512,512]{1,0:T(8,128)} %inv_hbm.1, f32[512,128]{1,0:T(8,128)} %one_hbm.1, f32[512,128]{1,0:T(8,128)} %two_hbm.1, bf16[1,256,256]{2,1,0:T(8,128)(2,1)} %coarse_hbm.1, bf16[2,256,256]{2,1,0:T(8,128)(2,1)} %fine_hbm.1), custom_call_target="tpu_custom_call" | custom-call | tf_op jit(solution)/shard_map/pallas_call | solution.py:440
  54.4 0.7 %copy.8 = f32[512,64]{0,1:T(8,128)} copy(f32[512,64]{0,1:T(8,128)S(1)} %bitcast.2) | data formatting | bytes 262144

commit v8 on v7

--- a/solution.py
+++ b/solution.py
@@ -59,14 +59,18 @@
     return sorted(steps, key=lambda step: -away(step[0], NZ) - away(step[1], NX))
 
 
-def local_products(inv, two, one, rhs_t, prod_ref, s_high_ref, s_low_ref, x_ref):
-    both = jnp.concatenate((two, one), axis=1)
-    both_high, both_low = split2(both)
-    inv_high, inv_low = split2(inv)
+def local_products(
+    inv_ref, two_ref, one_ref, rhs_ref, loads, prod_ref, s_high_ref, s_low_ref, x_ref
+):
+    for load in loads[1:]:
+        load.wait()
+    both_high, both_low = split2(jnp.concatenate((two_ref[...], one_ref[...]), axis=1))
+    rhs_high, rhs_low = split2(rhs_ref[...])
+    loads[0].wait()
+    inv_high, inv_low = split2(inv_ref[...])
     solved = dot(inv_high, both_high, NN) + (
         dot(inv_high, both_low, NN) + dot(inv_low, both_high, NN)
     )
-    rhs_high, rhs_low = split2(rhs_t)
     x_t = dot(rhs_high, inv_high, NN) + (
         dot(rhs_high, inv_low, NN) + dot(rhs_low, inv_high, NN)
     )
@@ -133,11 +137,8 @@
     for peer in peers:
         pl.semaphore_signal(barrier, inc=1, device_id=peer, device_id_type=MESH)
 
-    for load in loads[:4]:
-        load.wait()
     local_products(
-        inv_ref[...], two_ref[...], one_ref[...], rhs_ref[...],
-        prod_ref, s_high_ref, s_low_ref, x_ref,
+        inv_ref, two_ref, one_ref, rhs_ref, loads[:4], prod_ref, s_high_ref, s_low_ref, x_ref
     )
     pl.semaphore_wait(barrier, len(peers))
 
@@ -316,7 +317,7 @@
         for j in range(k + 1, 16):
             across = row_of(cols[j][at], sub)
             if j == k + 1:
-                cols[j] = [cols[j][t] - (raw[t] * across * guess) * refine for t in range(2)]
+                cols[j] = [cols[j][t] - raw[t] * guess * across * refine for t in range(2)]
             else:
                 cols[j] = [cols[j][t] - factors[t] * across for t in range(2)]
         across = row_of(tiles[at], sub)

time: 55.2 us -> 55.1 us (level)
  no operation moved by 1% of the time
where the time goes in v8:
time: 55.1 us; the launch traced here: 55 us
  Pallas kernels  54.3 us (99%)
  local copies, waits for them, and re-layouts  0.66 us (1%)
    pallas_call x1, Pallas kernels, body(): pl.pallas_call(whole_kernel, out_shape=shape(64, rows), in_specs=[hbm] *...  54.3 us

profile of v8, /device:TPU:1, one launch (start us, length us, event | category | flops | bytes accessed | tf_op | source)
XLA Modules:
  0.0 55.0 jit_solution(7965777489496399395)
XLA Ops:
  0.0 54.3 %shard_map.64 = f32[64,512]{1,0:T(8,128)S(1)} custom-call(f32[64,512]{1,0:T(8,128)} %bitcast.3, f32[512,512]{1,0:T(8,128)} %inv_hbm.1, f32[512,128]{1,0:T(8,128)} %one_hbm.1, f32[512,128]{1,0:T(8,128)} %two_hbm.1, bf16[1,256,256]{2,1,0:T(8,128)(2,1)} %coarse_hbm.1, bf16[2,256,256]{2,1,0:T(8,128)(2,1)} %fine_hbm.1), custom_call_target="tpu_custom_call" | custom-call | tf_op jit(solution)/shard_map/pallas_call | solution.py:441
  54.3 0.7 %copy.8 = f32[512,64]{0,1:T(8,128)} copy(f32[512,64]{0,1:T(8,128)S(1)} %bitcast.2) | data formatting | bytes 262144
